TPU v7x, 64 devices: a 2x2x8 block of a 4x4x8 slice. The times are simulated.
64 devices in a mesh: data: 4 (over x, y), dap: 16 (over z, core).
Axes of the slice: x: 2, y: 2, z: 8, core: 2. Of those that a mesh axis runs over, the one named last changes fastest.
The devices are a block of a 4x4x8 slice.
Arguments:
- msa_act: bfloat16 [8, 64, 192, 256], P('data', 'dap'), parts along dimension 0
- pair_act: bfloat16 [8, 192, 192, 128], P('data', 'dap'), parts along dimension 0
- msa_mask: int32 [8, 64, 192], P('data'), parts along dimension 0
- res_mask: int32 [8, 192], P('data'), parts along dimension 0
- w_row_bias: bfloat16 [128, 8], replicated
- w_row_qkvg: bfloat16 [256, 4, 8, 32], replicated
- w_row_out: bfloat16 [8, 32, 256], replicated
- w_col_qkvg: bfloat16 [256, 4, 8, 32], replicated
- w_col_out: bfloat16 [8, 32, 256], replicated
- w_opm_ac: bfloat16 [256, 2, 32], replicated
- w_opm_out: bfloat16 [32, 32, 128], replicated
- w_ts_bias: bfloat16 [128, 4], replicated
- w_ts_qkvg: bfloat16 [128, 4, 4, 32], replicated
- w_ts_out: bfloat16 [4, 32, 128], replicated
- w_te_bias: bfloat16 [128, 4], replicated
- w_te_qkvg: bfloat16 [128, 4, 4, 32], replicated
- w_te_out: bfloat16 [4, 32, 128], replicated
Outputs:
- output 1: bfloat16 [8, 64, 192, 256], P('data', 'dap'), parts along dimension 0
- output 2: bfloat16 [8, 192, 192, 128], P('data', 'dap'), parts along dimension 0
There are 4 independent parts. A program takes and returns all parts, laid end to end along the dimension named above; an argument that names none is the same for every part.
All inputs are finite; a program needn't handle non-finite values.
Results may differ from a plain program's by a relative error of at most 0.0158742.
Values are sent between devices in bfloat16 or wider.
A program may use at most 768 MiB of HBM per device.

v0:
```python
import jax
import jax.numpy as jnp
from jax import lax
from jax.sharding import PartitionSpec as P

SCORE_ELEMS = 8388608
MASK_SCALE = 10000.0
LN_EPS = 1e-5
OPM_EPS = 1e-3
N_WEIGHTS = 13
PART_AXIS = 'data'
GROUP_AXIS = 'dap'


def layer_norm(tensor):
    x_float = tensor.astype(jnp.float32)
    mean_val = jnp.mean(x_float, axis=-1, keepdims=True)
    centred = x_float - mean_val
    var_val = jnp.mean(centred * centred, axis=-1, keepdims=True)
    return (centred * lax.rsqrt(var_val + LN_EPS)).astype(jnp.bfloat16)


def mask_to_bias(mask):
    return (mask.astype(jnp.float32) - 1.0) * MASK_SCALE


def rows_per_map(n_rows, per_row):
    return max(1, min(n_rows, SCORE_ELEMS // per_row))


def gated_attention(x_row, normed, key_bias, pair_bias, w_qkvg, w_out):
    proj_all = jnp.einsum('lc,cghd->glhd', normed, w_qkvg, preferred_element_type=jnp.float32)
    queries = proj_all[0].astype(jnp.bfloat16)
    keys_bf = proj_all[1].astype(jnp.bfloat16)
    values_bf = proj_all[2].astype(jnp.bfloat16)
    gate_sig = jax.nn.sigmoid(proj_all[3])
    inv_sqrt = queries.shape[-1] ** -0.5
    logits = jnp.einsum('qhd,khd->hqk', queries, keys_bf, preferred_element_type=jnp.float32) * inv_sqrt + key_bias
    if pair_bias is not None:
        logits = logits + pair_bias
    attn_prob = jax.nn.softmax(logits, axis=-1).astype(jnp.bfloat16)
    mixed = jnp.einsum('hqk,khd->qhd', attn_prob, values_bf, preferred_element_type=jnp.float32) * gate_sig
    update = jnp.einsum('qhd,hdc->qc', mixed.astype(jnp.bfloat16), w_out, preferred_element_type=jnp.float32)
    return (x_row.astype(jnp.float32) + update).astype(jnp.bfloat16)


def attend_rows(row_stack, normed, key_rows, pair_bias, w_qkvg, w_out):
    n_rows = row_stack.shape[0]
    length = row_stack.shape[1]
    n_heads = w_qkvg.shape[2]
    return lax.map(lambda row_in: gated_attention(row_in[0], row_in[1], row_in[2], pair_bias, w_qkvg, w_out),
                   (row_stack, normed, key_rows), batch_size=rows_per_map(n_rows, n_heads * length * length))


def gathered_bias(normed, w_bias):
    bias_part = jnp.einsum('ijc,ch->hij', normed, w_bias, preferred_element_type=jnp.float32).astype(jnp.bfloat16)
    return lax.all_gather(bias_part, GROUP_AXIS, axis=1, tiled=True)


def triangle_rows(pair_rows, res_mask, w_bias, w_qkvg, w_out):
    normed = layer_norm(pair_rows)
    key_rows = jnp.broadcast_to(mask_to_bias(res_mask)[None, :], (pair_rows.shape[0], res_mask.shape[0]))
    return attend_rows(pair_rows, normed, key_rows, gathered_bias(normed, w_bias), w_qkvg, w_out)


def outer_rows(pair_rows, left_proj, right_proj, norm_pairs, w_opm_out):
    n_rows = pair_rows.shape[0]
    n_res = right_proj.shape[0]
    width = right_proj.shape[2]

    def one_row(row_in):
        left_row, norm_row, pair_row = row_in
        outer = jnp.einsum('se,jsf->jef', left_row, right_proj, preferred_element_type=jnp.float32)
        outer = outer / (norm_row[:, None, None] + OPM_EPS)
        update = jnp.einsum('jef,efc->jc', outer.astype(jnp.bfloat16), w_opm_out, preferred_element_type=jnp.float32)
        return (pair_row.astype(jnp.float32) + update).astype(jnp.bfloat16)

    return lax.map(one_row, (left_proj, norm_pairs, pair_rows), batch_size=rows_per_map(n_rows, n_res * width * width))


def crop_block(piece_d8, pair_rows, local_c8, res_mask, weights):
    (w_row_bias, w_row_qkvg, w_row_out, w_col_qkvg, w_col_out, w_opm_ac, w_opm_out,
     w_ts_bias, w_ts_qkvg, w_ts_out, w_te_bias, w_te_qkvg, w_te_out) = weights
    dev_index = lax.axis_index(GROUP_AXIS)
    seq_local = piece_d8.shape[0]
    res_local = pair_rows.shape[0]
    row_bias = gathered_bias(layer_norm(pair_rows), w_row_bias)
    seq_mask = lax.dynamic_slice_in_dim(local_c8, dev_index * seq_local, seq_local, axis=0)
    piece_d8 = attend_rows(piece_d8, layer_norm(piece_d8), mask_to_bias(seq_mask), row_bias, w_row_qkvg, w_row_out)
    value_a8 = jnp.swapaxes(lax.all_to_all(piece_d8, GROUP_AXIS, 1, 0, tiled=True), 0, 1)
    col_mask = jnp.swapaxes(lax.dynamic_slice_in_dim(local_c8, dev_index * res_local, res_local, axis=1), 0, 1)
    value_a8 = attend_rows(value_a8, layer_norm(value_a8), mask_to_bias(col_mask), None, w_col_qkvg, w_col_out)
    col_mask_bf = col_mask.astype(jnp.bfloat16)
    proj_ac = jnp.einsum('isc,cpe->pise', layer_norm(value_a8), w_opm_ac,
                         preferred_element_type=jnp.float32).astype(jnp.bfloat16)
    left_proj = proj_ac[0] * col_mask_bf[:, :, None]
    right_proj = lax.all_gather(proj_ac[1] * col_mask_bf[:, :, None], GROUP_AXIS, axis=0, tiled=True)
    norm_pairs = jnp.dot(col_mask_bf, local_c8.astype(jnp.bfloat16), preferred_element_type=jnp.float32)
    pair_rows = outer_rows(pair_rows, left_proj, right_proj, norm_pairs, w_opm_out)
    pair_rows = triangle_rows(pair_rows, res_mask, w_ts_bias, w_ts_qkvg, w_ts_out)
    pair_cols = jnp.swapaxes(lax.all_to_all(pair_rows, GROUP_AXIS, 1, 0, tiled=True), 0, 1)
    pair_cols = triangle_rows(pair_cols, res_mask, w_te_bias, w_te_qkvg, w_te_out)
    pair_out = lax.all_to_all(jnp.swapaxes(pair_cols, 0, 1), GROUP_AXIS, 0, 1, tiled=True)
    local_c7 = jnp.swapaxes(lax.all_to_all(value_a8, GROUP_AXIS, 1, 0, tiled=True), 0, 1)
    return local_c7, pair_out


def solution(mesh):
    rows_spec = P(PART_AXIS, GROUP_AXIS, None, None)
    in_specs = (rows_spec, rows_spec, P(PART_AXIS, None, None), P(PART_AXIS, None)) + (P(),) * N_WEIGHTS

    def local_block(value_a7, pair_act, local_c8, res_mask, *weights):
        array_b8 = []
        pair_list = []
        for crop_idx in range(value_a7.shape[0]):
            array_b7, pair_new = crop_block(value_a7[crop_idx], pair_act[crop_idx], local_c8[crop_idx],
                                           res_mask[crop_idx], weights)
            array_b8.append(array_b7)
            pair_list.append(pair_new)
        return jnp.stack(array_b8), jnp.stack(pair_list)

    return jax.shard_map(local_block, mesh=mesh, in_specs=in_specs, out_specs=(rows_spec, rows_spec),
                         check_vma=False)
```

profile of v0, /device:TPU:21, one launch (start us, length us, event | category | flops | bytes accessed | tf_op | source)
XLA Modules:
  0.0 479.9 jit_solution(6547048713673012598)
XLA Ops:
  0.7 1.6 convert_reduce_fusion.7
  2.3 1.7 fusion.204
  4.0 1.7 convert_reduce_fusion.3
  5.8 1.7 fusion.162
  8.6 24.8 %all_gather.25 = bf16[8,192,192]{2,0,1:T(8,128)(2,1)S(1)} all-gather(bf16[8,12,192]{2,0,1:T(8,128)(2,1)S(1)} %fusion.167), channel_id=1, replica_groups=mesh['data'=4,'dap'=16] {'dap'}, dimensions={1}, use_global_device_ids=true | all-gather | bytes 626688 | tf_op jit(solution)/shard_map/all_gather | solution.py:57
  33.4 1.8 copy.115
  35.2 3.5 fusion.335
  38.8 7.0 %fusion.336 = (f32[4,8,192]{2,1,0:T(8,128)S(1)}, f32[4,8,192,192]{2,3,1,0:T(8,128)}) fusion(f32[8,192,192]{1,2,0:T(8,128)} %copy.115, f32[4,192]{1,0:T(4,128)S(1)} %multiply_bitcast_fusion.2, bf16[4,4,192,8,32]{2,4,3,1,0:T(8,128)(2,1)} %get-tuple-element.188), kind=kOutput, calls=%fused_computation.444 | convolution fusion | flops 81395904 | bytes 7367680 | tf_op jit(solution)/shard_map/while/body/eval_jaxpr/vmap()/sub | solution.py:41
  45.8 4.2 fusion.154
  51.0 4.3 all-to-all-start.2
  56.6 24.3 %all_gather.24 = bf16[8,192,192]{2,0,1:T(8,128)(2,1)S(1)} all-gather(bf16[8,12,192]{2,0,1:T(8,128)(2,1)S(1)} %fusion.166), channel_id=1, replica_groups=mesh['data'=4,'dap'=16] {'dap'}, dimensions={1}, use_global_device_ids=true | all-gather | bytes 626688 | tf_op jit(solution)/shard_map/all_gather | solution.py:57
  80.9 1.8 copy.107
  82.7 3.5 fusion.339
  86.2 7.0 %fusion.340 = (f32[4,8,192]{2,1,0:T(8,128)S(1)}, f32[4,8,192,192]{2,3,1,0:T(8,128)}) fusion(f32[8,192,192]{1,2,0:T(8,128)} %copy.107, f32[4,192]{1,0:T(4,128)S(1)} %multiply_bitcast_fusion.3, bf16[4,4,192,8,32]{2,4,3,1,0:T(8,128)(2,1)} %get-tuple-element.203), kind=kOutput, calls=%fused_computation.448 | convolution fusion | flops 81395904 | bytes 7367680 | tf_op jit(solution)/shard_map/while/body/eval_jaxpr/vmap()/sub | solution.py:41
  93.2 4.3 fusion.155
  99.4 6.2 %all-to-all-start = ((bf16[4,192,256]{2,0,1:T(4,128)(2,1)}), bf16[4,192,256]{2,0,1:T(4,128)(2,1)}, u32[]{:S(2)}, u32[]{:S(2)}) async-start(bf16[4,192,256]{2,0,1:T(4,128)(2,1)} %copy.109), calls=%async_computation | async-start | bytes 786432 | tf_op jit(solution)/shard_map/all_to_all | solution.py:90
  107.8 11.5 %all-to-all-done = bf16[4,192,256]{2,0,1:T(4,128)(2,1)} async-done(((bf16[4,192,256]{2,0,1:T(4,128)(2,1)}), bf16[4,192,256]{2,0,1:T(4,128)(2,1)}, u32[]{:S(2)}, u32[]{:S(2)}) %all-to-all-start) | async-done | bytes 393248 | tf_op jit(solution)/shard_map/all_to_all | solution.py:90
  121.6 1.4 reshape.406
  123.6 3.8 fusion.341
  127.3 1.6 copy-done.3
  129.6 3.6 fusion.342
  133.2 4.1 convert_reduce_fusion.5
  137.4 2.0 copy.113
  139.4 1.3 fusion.200
  140.7 1.4 fusion.164
  142.2 19.5 %all_gather.26 = bf16[192,64,32]{1,2,0:T(8,128)(2,1)} all-gather(bf16[12,64,32]{1,2,0:T(8,128)(2,1)S(1)} %fusion.291), channel_id=1, replica_groups=mesh['data'=4,'dap'=16] {'dap'}, dimensions={0}, use_global_device_ids=true | all-gather | bytes 835584 | tf_op jit(solution)/shard_map/all_gather | solution.py:97
  161.7 4.8 convert_reduce_fusion.1
  168.3 4.4 fusion.355
  172.7 3.8 fusion.337
  176.4 1.7 copy-done.4
  178.7 3.0 fusion.338
  181.7 3.5 convert_reduce_fusion.4
  187.0 22.0 %all_gather.29 = bf16[192,64,32]{1,2,0:T(8,128)(2,1)} all-gather(bf16[12,64,32]{1,2,0:T(8,128)(2,1)S(1)} %fusion.286), channel_id=1, replica_groups=mesh['data'=4,'dap'=16] {'dap'}, dimensions={0}, use_global_device_ids=true | all-gather | bytes 835584 | tf_op jit(solution)/shard_map/all_gather | solution.py:97
  209.0 4.7 convert_reduce_fusion
  215.6 4.5 fusion.347
  220.1 15.6 %all_gather.27 = bf16[4,192,192]{2,0,1:T(4,128)(2,1)S(1)} all-gather(bf16[4,12,192]{2,0,1:T(4,128)(2,1)S(1)} %fusion.168), channel_id=1, replica_groups=mesh['data'=4,'dap'=16] {'dap'}, dimensions={1}, use_global_device_ids=true | all-gather | bytes 313344 | tf_op jit(solution)/shard_map/all_gather | solution.py:57
  236.1 8.9 %fusion.356 = (f32[12,4,192]{2,1,0:T(4,128)S(1)}, f32[12,4,192,192]{2,3,1,0:T(8,128)}) fusion(f32[4,192,192]{1,2,0:T(8,128)S(1)} %copy.128, f32[192]{0:T(256)S(1)} %bitcast.836, bf16[12,4,192,4,32]{2,4,3,1,0:T(8,128)(2,1)} %get-tuple-element.256), kind=kOutput, calls=%fused_computation.456 | convolution fusion | flops 122093760 | bytes 9278208 | tf_op jit(solution)/shard_map/while/body/eval_jaxpr/vmap()/sub | solution.py:41
  245.0 5.7 %fusion.144 = bf16[12,192,128]{2,1,0:T(8,128)(2,1)S(1)} fusion(bf16[12,192,128]{2,1,0:T(8,128)(2,1)S(1)} %get-tuple-element.247, f32[12,4,192,4,32]{2,4,3,1,0:T(8,128)} %get-tuple-element.257, f32[12,4,192,192]{2,3,1,0:T(8,128)} %get-tuple-element.259, f32[12,4,192]{2,1,0:T(4,128)S(1)} %get-tuple-element.258, ...), kind=kOutput, calls=%fused_computation.168 | convolution fusion | flops 194641920 | bytes 13045760 | tf_op jit(solution)/shard_map/while/body/eval_jaxpr/vmap(qhd,hdc->qc)/dot_general | solution.py:43
  252.0 4.3 all-to-all-start.4
  256.3 32.2 %all_gather.30 = bf16[4,192,192]{2,0,1:T(4,128)(2,1)S(1)} all-gather(bf16[4,12,192]{2,0,1:T(4,128)(2,1)S(1)} %fusion.170), channel_id=1, replica_groups=mesh['data'=4,'dap'=16] {'dap'}, dimensions={1}, use_global_device_ids=true | all-gather | bytes 313344 | tf_op jit(solution)/shard_map/all_gather | solution.py:57
  288.9 8.9 %fusion.348 = (f32[12,4,192]{2,1,0:T(4,128)S(1)}, f32[12,4,192,192]{2,3,1,0:T(8,128)}) fusion(f32[4,192,192]{1,2,0:T(8,128)S(1)} %copy.144, f32[192]{0:T(256)S(1)} %bitcast.834, bf16[12,4,192,4,32]{2,4,3,1,0:T(8,128)(2,1)} %get-tuple-element.229), kind=kOutput, calls=%fused_computation.452 | convolution fusion | flops 122093760 | bytes 9278208 | tf_op jit(solution)/shard_map/while/body/eval_jaxpr/vmap()/sub | solution.py:41
  297.9 5.8 %fusion.145 = bf16[12,192,128]{2,1,0:T(8,128)(2,1)S(1)} fusion(bf16[12,192,128]{2,1,0:T(8,128)(2,1)S(1)} %copy-done.7, f32[12,4,192,4,32]{2,4,3,1,0:T(8,128)} %get-tuple-element.230, f32[12,4,192,192]{2,3,1,0:T(8,128)} %get-tuple-element.232, f32[12,4,192]{2,1,0:T(4,128)S(1)} %get-tuple-element.231, bf16[12,4,192,4,32]{2,4,3,1,0:T(8,128)(2,1)} %get-tuple-element.229, ...), kind=kOutput, calls=%fused_computation.169 | convolution fusion | flops 194641920 | bytes 13045760 | tf_op jit(solution)/shard_map/while/body/eval_jaxpr/vmap(qhd,hdc->qc)/dot_general | solution.py:43
  304.9 6.0 %all-to-all-start.6 = ((bf16[12,192,128]{2,0,1:T(8,128)(2,1)}), bf16[12,192,128]{2,0,1:T(8,128)(2,1)}, u32[]{:S(2)}, u32[]{:S(2)}) async-start(bf16[12,192,128]{2,0,1:T(8,128)(2,1)} %copy.146), calls=%async_computation.6 | async-start | bytes 1572864 | tf_op jit(solution)/shard_map/all_to_all | solution.py:101
  311.2 1.9 copy.132
  313.1 1.4 reshape.404
  316.9 26.3 %all_gather.28 = bf16[4,192,192]{2,0,1:T(4,128)(2,1)S(1)} all-gather(bf16[4,12,192]{2,0,1:T(4,128)(2,1)S(1)} %fusion.169), channel_id=1, replica_groups=mesh['data'=4,'dap'=16] {'dap'}, dimensions={1}, use_global_device_ids=true | all-gather | bytes 313344 | tf_op jit(solution)/shard_map/all_gather | solution.py:57
  344.5 4.4 fusion.357
  348.9 6.6 %all-to-all-start.1 = ((bf16[12,64,256]{2,0,1:T(8,128)(2,1)}), bf16[12,64,256]{2,0,1:T(8,128)(2,1)S(1)}, u32[]{:S(2)}, u32[]{:S(2)}) async-start(bf16[12,64,256]{2,0,1:T(8,128)(2,1)} %copy.113), calls=%async_computation.1 | async-start | bytes 1048576 | tf_op jit(solution)/shard_map/all_to_all | solution.py:104
  358.0 3.3 copy.148
  361.3 1.4 reshape.405
  364.1 9.7 %fusion.358 = (f32[12,4,192]{2,1,0:T(4,128)}, f32[12,4,192,192]{2,3,1,0:T(8,128)}) fusion(f32[4,192,192]{1,2,0:T(8,128)} %copy.134, f32[192]{0:T(256)S(1)} %bitcast.837, bf16[12,4,192,4,32]{2,4,3,1,0:T(8,128)(2,1)} %get-tuple-element.260), kind=kOutput, calls=%fused_computation.458 | convolution fusion | flops 122093760 | bytes 9474816 | tf_op jit(solution)/shard_map/while/body/eval_jaxpr/vmap()/sub | solution.py:41
  373.8 5.7 %fusion.133 = bf16[192,12,128]{2,0,1:T(8,128)(2,1)S(1)} fusion(f32[192,12,128]{2,0,1:T(8,128)S(1)} %reshape.404, f32[12,4,192,4,32]{2,4,3,1,0:T(8,128)} %get-tuple-element.261, f32[12,4,192,192]{2,3,1,0:T(8,128)} %get-tuple-element.263, f32[12,4,192]{2,1,0:T(4,128)} %get-tuple-element.262, bf16[12,4,192,4,32]{2,4,3,1,0:T(8,128)(2,1)} %get-tuple-element.260, ...), kind=kOutput, calls=%fused_computation.165 | convolution fusion | flops 194347008 | bytes 13647872 | tf_op jit(solution)/shard_map/while/body/eval_jaxpr/vmap(qhd,hdc->qc)/dot_general | solution.py:43
  380.5 1.3 copy.136
  381.8 18.3 %all_gather.31 = bf16[4,192,192]{2,0,1:T(4,128)(2,1)S(1)} all-gather(bf16[4,12,192]{2,0,1:T(4,128)(2,1)S(1)} %fusion.171), channel_id=1, replica_groups=mesh['data'=4,'dap'=16] {'dap'}, dimensions={1}, use_global_device_ids=true | all-gather | bytes 313344 | tf_op jit(solution)/shard_map/all_gather | solution.py:57
  400.1 5.3 %fusion.349 = (bf16[12,4,192,4,32]{2,4,3,1,0:T(8,128)(2,1)}, f32[12,4,192,4,32]{2,4,3,1,0:T(8,128)}) fusion(bf16[128,4,4,32]{0,3,2,1:T(8,128)(2,1)} %param.32, f32[12,192]{1,0:T(8,128)S(1)} %add_rsqrt_fusion, f32[12,192]{1,0:T(8,128)S(1)} %broadcast_multiply_fusion, f32[192,12,128]{2,0,1:T(8,128)S(1)} %reshape.405), kind=kOutput, calls=%fused_computation.453 | convolution fusion | flops 304054272 | bytes 8407040 | tf_op jit(solution)/shard_map/while/body/eval_jaxpr/vmap(lc,cghd->glhd)/dot_general | solution.py:32
  405.4 5.3 %all-to-all-start.3 = ((bf16[12,64,256]{2,0,1:T(8,128)(2,1)}), bf16[12,64,256]{2,0,1:T(8,128)(2,1)S(1)}, u32[]{:S(2)}, u32[]{:S(2)}) async-start(bf16[12,64,256]{2,0,1:T(8,128)(2,1)} %copy.121), calls=%async_computation.3 | async-start | bytes 1048576 | tf_op jit(solution)/shard_map/all_to_all | solution.py:104
  412.0 9.1 %fusion.350 = (f32[12,4,192]{2,1,0:T(4,128)S(1)}, f32[12,4,192,192]{2,3,1,0:T(8,128)}) fusion(f32[4,192,192]{1,2,0:T(8,128)} %copy.150, f32[192]{0:T(256)S(1)} %bitcast.835, bf16[12,4,192,4,32]{2,4,3,1,0:T(8,128)(2,1)} %get-tuple-element.240), kind=kOutput, calls=%fused_computation.454 | convolution fusion | flops 122093760 | bytes 9474816 | tf_op jit(solution)/shard_map/while/body/eval_jaxpr/vmap()/sub | solution.py:41
  421.1 5.5 %all-to-all-done.3 = bf16[12,64,256]{2,0,1:T(8,128)(2,1)S(1)} async-done(((bf16[12,64,256]{2,0,1:T(8,128)(2,1)}), bf16[12,64,256]{2,0,1:T(8,128)(2,1)S(1)}, u32[]{:S(2)}, u32[]{:S(2)}) %all-to-all-start.3) | async-done | bytes 393248 | tf_op jit(solution)/shard_map/all_to_all | solution.py:104
  426.7 3.8 all-to-all-start.5
  430.5 6.5 %fusion.132 = bf16[192,12,128]{2,0,1:T(8,128)(2,1)} fusion(f32[192,12,128]{2,0,1:T(8,128)S(1)} %reshape.405, f32[12,4,192,4,32]{2,4,3,1,0:T(8,128)} %get-tuple-element.241, f32[12,4,192,192]{2,3,1,0:T(8,128)} %get-tuple-element.243, f32[12,4,192]{2,1,0:T(4,128)S(1)} %get-tuple-element.242, bf16[12,4,192,4,32]{2,4,3,1,0:T(8,128)(2,1)} %get-tuple-element.240, ...), kind=kOutput, calls=%fused_computation.164 | convolution fusion | flops 194347008 | bytes 13635584 | tf_op jit(solution)/shard_map/while/body/eval_jaxpr/vmap(qhd,hdc->qc)/dot_general | solution.py:43
  437.0 2.3 copy.152
  439.4 12.8 %all-to-all-done.5 = bf16[192,12,128]{2,1,0:T(8,128)(2,1)S(1)} async-done(((bf16[192,12,128]{2,1,0:T(8,128)(2,1)}), bf16[192,12,128]{2,1,0:T(8,128)(2,1)S(1)}, u32[]{:S(2)}, u32[]{:S(2)}) %all-to-all-start.5) | async-done | bytes 589856 | tf_op jit(solution)/shard_map/all_to_all | solution.py:103
  452.2 4.0 all-to-all-start.7
  459.2 18.8 %all-to-all-done.7 = bf16[192,12,128]{2,1,0:T(8,128)(2,1)S(1)} async-done(((bf16[192,12,128]{2,1,0:T(8,128)(2,1)}), bf16[192,12,128]{2,1,0:T(8,128)(2,1)S(1)}, u32[]{:S(2)}, u32[]{:S(2)}) %all-to-all-start.7) | async-done | bytes 589856 | tf_op jit(solution)/shard_map/all_to_all | solution.py:103
  (137 shorter events, 34.7 us)
Async XLA Ops:
  0.6 34.6 %copy-start = (bf16[256,4,8,32]{0,3,2,1:T(8,128)(2,1)S(1)}, bf16[256,4,8,32]{0,3,2,1:T(8,128)(2,1)}, u32[]{:S(2)}) copy-start(bf16[256,4,8,32]{0,3,2,1:T(8,128)(2,1)} %param.22) | copy-start | bytes 1572868
  0.6 5.2 %copy-start.5 = (bf16[2,12,192,128]{3,2,1,0:T(8,128)(2,1)S(1)}, bf16[2,12,192,128]{3,2,1,0:T(8,128)(2,1)}, u32[]{:S(2)}) copy-start(bf16[2,12,192,128]{3,2,1,0:T(8,128)(2,1)} %param.18) | copy-start | bytes 3538948
  0.7 6.9 %copy-start.12 = (s32[2,64,192]{2,1,0:T(8,128)S(1)}, s32[2,64,192]{2,1,0:T(8,128)}, u32[]{:S(2)}) copy-start(s32[2,64,192]{2,1,0:T(8,128)} %param.19) | copy-start | bytes 294916
  0.7 6.9 %copy-start.22 = (bf16[128,8]{0,1:T(8,128)(2,1)S(1)}, bf16[128,8]{0,1:T(8,128)(2,1)}, u32[]{:S(2)}) copy-start(bf16[128,8]{0,1:T(8,128)(2,1)} %param.21) | copy-start | bytes 6148
  5.8 29.4 %copy-start.2 = (bf16[2,4,192,256]{3,2,1,0:T(8,128)(2,1)S(1)}, bf16[2,4,192,256]{3,2,1,0:T(8,128)(2,1)}, u32[]{:S(2)}) copy-start(bf16[2,4,192,256]{3,2,1,0:T(8,128)(2,1)} %param.17) | copy-start | bytes 2359300
  38.7 7.0 %copy-start.15 = (bf16[8,32,256]{2,1,0:T(8,128)(2,1)S(1)}, bf16[8,32,256]{2,1,0:T(8,128)(2,1)}, u32[]{:S(2)}) copy-start(bf16[8,32,256]{2,1,0:T(8,128)(2,1)} %param.23) | copy-start | bytes 393220
  51.0 48.4 %all-to-all-start.2 = ((bf16[4,192,256]{2,0,1:T(4,128)(2,1)}), bf16[4,192,256]{2,0,1:T(4,128)(2,1)}, u32[]{:S(2)}, u32[]{:S(2)}) async-start(bf16[4,192,256]{2,0,1:T(4,128)(2,1)} %copy.117), calls=%async_computation.2 | async-start | bytes 786432 | tf_op jit(solution)/shard_map/all_to_all | solution.py:90
  86.2 7.0 %copy-start.16 = (bf16[8,32,256]{2,1,0:T(8,128)(2,1)S(1)}, bf16[8,32,256]{2,1,0:T(8,128)(2,1)}, u32[]{:S(2)}) copy-start(bf16[8,32,256]{2,1,0:T(8,128)(2,1)} %param.23) | copy-start | bytes 393220
  93.2 5.7 %copy-start.14 = (s32[2,192]{1,0:T(2,128)S(1)}, s32[2,192]{1,0:T(2,128)}, u32[]{:S(2)}) copy-start(s32[2,192]{1,0:T(2,128)} %param.20) | copy-start | bytes 4612
  99.4 19.9 %all-to-all-start = ((bf16[4,192,256]{2,0,1:T(4,128)(2,1)}), bf16[4,192,256]{2,0,1:T(4,128)(2,1)}, u32[]{:S(2)}, u32[]{:S(2)}) async-start(bf16[4,192,256]{2,0,1:T(4,128)(2,1)} %copy.109), calls=%async_computation | async-start | bytes 786432 | tf_op jit(solution)/shard_map/all_to_all | solution.py:90
  107.8 15.8 %copy-start.9 = (bf16[256,4,8,32]{0,3,2,1:T(8,128)(2,1)S(1)}, bf16[256,4,8,32]{0,3,2,1:T(8,128)(2,1)}, u32[]{:S(2)}) copy-start(bf16[256,4,8,32]{0,3,2,1:T(8,128)(2,1)} %param.24) | copy-start | bytes 1572868
  127.3 1.6 copy-start.3
  129.6 3.6 copy-start.17
  161.7 5.6 %copy-start.23 = (bf16[128,4]{0,1:T(4,128)(2,1)S(1)}, bf16[128,4]{0,1:T(4,128)(2,1)}, u32[]{:S(2)}) copy-start(bf16[128,4]{0,1:T(4,128)(2,1)} %param.28) | copy-start | bytes 3076
  161.7 6.6 %copy-start.10 = (bf16[128,4,4,32]{0,3,2,1:T(8,128)(2,1)S(1)}, bf16[128,4,4,32]{0,3,2,1:T(8,128)(2,1)}, u32[]{:S(2)}) copy-start(bf16[128,4,4,32]{0,3,2,1:T(8,128)(2,1)} %param.29) | copy-start | bytes 393220
  176.4 1.7 copy-start.4
  178.7 3.0 copy-start.18
  181.7 4.9 %copy-start.19 = (bf16[256,2,32]{0,2,1:T(8,128)(2,1)S(1)}, bf16[256,2,32]{0,2,1:T(8,128)(2,1)}, u32[]{:S(2)}) copy-start(bf16[256,2,32]{0,2,1:T(8,128)(2,1)} %param.26) | copy-start | bytes 98308
  213.7 6.4 %copy-start.6 = (bf16[12,192,128]{2,1,0:T(8,128)(2,1)}, bf16[12,192,128]{2,1,0:T(8,128)(2,1)S(1)}, u32[]{:S(2)}) copy-start(bf16[12,192,128]{2,1,0:T(8,128)(2,1)S(1)} %get-tuple-element.228) | copy-start | bytes 1769476
  236.1 8.9 %copy-start.20 = (bf16[4,32,128]{2,1,0:T(8,128)(2,1)S(1)}, bf16[4,32,128]{2,1,0:T(8,128)(2,1)}, u32[]{:S(2)}) copy-start(bf16[4,32,128]{2,1,0:T(8,128)(2,1)} %param.30) | copy-start | bytes 98308
  252.0 52.9 %all-to-all-start.4 = ((bf16[12,192,128]{2,0,1:T(8,128)(2,1)}), bf16[12,192,128]{2,0,1:T(8,128)(2,1)S(1)}, u32[]{:S(2)}, u32[]{:S(2)}) async-start(bf16[12,192,128]{2,0,1:T(8,128)(2,1)} %copy.130), calls=%async_computation.4 | async-start | bytes 1572864 | tf_op jit(solution)/shard_map/all_to_all | solution.py:101
  288.9 9.0 %copy-start.7 = (bf16[12,192,128]{2,1,0:T(8,128)(2,1)S(1)}, bf16[12,192,128]{2,1,0:T(8,128)(2,1)}, u32[]{:S(2)}) copy-start(bf16[12,192,128]{2,1,0:T(8,128)(2,1)} %copy-done.6) | copy-start | bytes 1769476
  304.9 43.9 %all-to-all-start.6 = ((bf16[12,192,128]{2,0,1:T(8,128)(2,1)}), bf16[12,192,128]{2,0,1:T(8,128)(2,1)}, u32[]{:S(2)}, u32[]{:S(2)}) async-start(bf16[12,192,128]{2,0,1:T(8,128)(2,1)} %copy.146), calls=%async_computation.6 | async-start | bytes 1572864 | tf_op jit(solution)/shard_map/all_to_all | solution.py:101
  313.1 2.8 copy-start.13
  314.5 29.9 %copy-start.11 = (bf16[128,4,4,32]{0,3,2,1:T(8,128)(2,1)S(1)}, bf16[128,4,4,32]{0,3,2,1:T(8,128)(2,1)}, u32[]{:S(2)}) copy-start(bf16[128,4,4,32]{0,3,2,1:T(8,128)(2,1)} %param.32) | copy-start | bytes 393220
  348.9 56.6 %all-to-all-start.1 = ((bf16[12,64,256]{2,0,1:T(8,128)(2,1)}), bf16[12,64,256]{2,0,1:T(8,128)(2,1)S(1)}, u32[]{:S(2)}, u32[]{:S(2)}) async-start(bf16[12,64,256]{2,0,1:T(8,128)(2,1)} %copy.113), calls=%async_computation.1 | async-start | bytes 1048576 | tf_op jit(solution)/shard_map/all_to_all | solution.py:104
  405.4 21.2 %all-to-all-start.3 = ((bf16[12,64,256]{2,0,1:T(8,128)(2,1)}), bf16[12,64,256]{2,0,1:T(8,128)(2,1)S(1)}, u32[]{:S(2)}, u32[]{:S(2)}) async-start(bf16[12,64,256]{2,0,1:T(8,128)(2,1)} %copy.121), calls=%async_computation.3 | async-start | bytes 1048576 | tf_op jit(solution)/shard_map/all_to_all | solution.py:104
  412.0 18.5 %copy-start.21 = (bf16[4,32,128]{2,1,0:T(8,128)(2,1)S(1)}, bf16[4,32,128]{2,1,0:T(8,128)(2,1)}, u32[]{:S(2)}) copy-start(bf16[4,32,128]{2,1,0:T(8,128)(2,1)} %param.33) | copy-start | bytes 98308
  426.7 25.5 %all-to-all-start.5 = ((bf16[192,12,128]{2,1,0:T(8,128)(2,1)}), bf16[192,12,128]{2,1,0:T(8,128)(2,1)S(1)}, u32[]{:S(2)}, u32[]{:S(2)}) async-start(bf16[192,12,128]{2,1,0:T(8,128)(2,1)} %copy.136), calls=%async_computation.5 | async-start | bytes 1572864 | tf_op jit(solution)/shard_map/all_to_all | solution.py:103
  452.2 25.8 %all-to-all-start.7 = ((bf16[192,12,128]{2,1,0:T(8,128)(2,1)}), bf16[192,12,128]{2,1,0:T(8,128)(2,1)S(1)}, u32[]{:S(2)}, u32[]{:S(2)}) async-start(bf16[192,12,128]{2,1,0:T(8,128)(2,1)} %copy.152), calls=%async_computation.7 | async-start | bytes 1572864 | tf_op jit(solution)/shard_map/all_to_all | solution.py:103
  458.1 21.4 %copy-start.1 = (bf16[256,4,8,32]{0,3,2,1:T(8,128)(2,1)S(1)}, bf16[256,4,8,32]{0,3,2,1:T(8,128)(2,1)}, u32[]{:S(2)}) copy-start(bf16[256,4,8,32]{0,3,2,1:T(8,128)(2,1)} %param.22) | copy-start | bytes 1572868
  459.2 19.1 %copy-start.8 = (bf16[1,12,192,128]{3,2,1,0:T(8,128)(2,1)S(1)}, bf16[1,12,192,128]{3,2,1,0:T(8,128)(2,1)}, u32[]{:S(2)}) copy-start(bf16[1,12,192,128]{3,2,1,0:T(8,128)(2,1)} %stack.21) | copy-start | bytes 1769476
where the time goes:
time: 488 us; the launch traced here: 480 us
  blocking collectives  183 us (38%)
  matrix products  143 us (29%)
  waiting for transfers between devices  48.6 us (10%)
  starting transfers between devices  40.6 us (8%)
  local copies, waits for them, and re-layouts  36.9 us (8%)
  other arithmetic  26.3 us (5%)
    all_gather x6, blocking collectives, gathered_bias(): return lax.all_gather(bias_part, GROUP_AXIS, axis=1, tiled=True)  142 us
    sub x6, matrix products, gated_attention(): attn_prob = jax.nn.softmax(logits, axis=-1).astype(jnp.bfloat16)  50.6 us
    all_gather x2, blocking collectives, crop_block(): lax.all_gather(proj_ac[1] * col_mask_bf[:, :, None], GROUP_AXIS, axis=0,...  41.5 us
    dot_general x8, matrix products, gated_attention(): jnp.einsum('qhd,hdc->qc', mixed.astype(jnp.bfloat16), w_out, preferred_el...  39.9 us
    dot_general x8, matrix products, gated_attention(): jnp.einsum('lc,cghd->glhd', normed, w_qkvg, preferred_element_type=jnp.fl...  33.1 us
    all_to_all x2, waiting for transfers between devices, crop_block(): lax.all_to_all(jnp.swapaxes(pair_cols, 0, 1), GROUP_AXIS, 0, 1, tiled=True)  31.6 us
    convert_element_type x18, local copies, waits for them, and re-layouts, gated_attention(): return (x_row.astype(jnp.float32) + update).astype(jnp.bfloat16)  23.7 us
    all_to_all x2, starting transfers between devices, crop_block(): lax.all_to_all(value_a8, GROUP_AXIS, 1, 0, tiled=True)  11.9 us
  transfers between devices with their start and end apart: 8, of which 4 were waited for; matrix products, arithmetic and copies ran while one was open for 22% of the time, Pallas kernels for 0%

commit v1 on v0

v1 whole, which is shorter than its diff:
```python
import functools
import math

import jax
import jax.numpy as jnp
import numpy as np
from jax import lax
from jax.experimental import pallas as pl
from jax.experimental.pallas import tpu as pltpu
from jax.sharding import PartitionSpec as P

MASK_SCALE = 10000.0
LN_EPS = 1e-5
OPM_EPS = 1e-3
LOG2E = math.log2(math.e)
N_WEIGHTS = 13
PART_AXIS = 'data'
GROUP_AXIS = 'dap'
MESH = pl.DeviceIdType.MESH
F32 = jnp.float32
BF16 = jnp.bfloat16
HD = 32
VMEM_BYTES = 60 * 1024 * 1024


def dot(a, b):
    return lax.dot_general(a, b, (((1,), (0,)), ((), ())), preferred_element_type=F32)


def dot_nt(a, b):
    return lax.dot_general(a, b, (((1,), (1,)), ((), ())), preferred_element_type=F32)


def dot_tn(a, b):
    return lax.dot_general(a, b, (((0,), (0,)), ((), ())), preferred_element_type=F32)


def layer_norm(x):
    x_float = x.astype(F32)
    centred = x_float - jnp.mean(x_float, axis=-1, keepdims=True)
    var = jnp.mean(centred * centred, axis=-1, keepdims=True)
    return (centred * lax.rsqrt(var + LN_EPS)).astype(BF16)


def sigmoid(x):
    return 1.0 / (1.0 + jnp.exp2(x * (-LOG2E)))


def iota(shape, dim):
    return lax.broadcasted_iota(jnp.int32, shape, dim)


def permutation(sizes, order, keep=None):
    total = int(np.prod(sizes))
    source = np.arange(total).reshape(sizes).transpose(order).reshape(-1)
    out = np.zeros((total, total), np.float32)
    out[np.arange(total), source] = 1.0
    return out


def softmax_cols(t):
    e = jnp.exp2(t - jnp.max(t, axis=0, keepdims=True))
    return (e * (1.0 / jnp.sum(e, axis=0, keepdims=True))).astype(BF16)


def pair_attention(y, w_t, w_out, bias_of):
    length, width = y.shape
    two = 2 * length
    scale = HD ** -0.5 * LOG2E
    y2 = jnp.concatenate([y, y], axis=0)
    q2 = dot_nt(w_t[0:width, :], y2)
    odd_head = (iota((width, two), 0) // HD) % 2
    right = (iota((width, two), 1) >= length).astype(jnp.int32)
    q2 = jnp.where(odd_head == right, q2, 0.0).astype(BF16)
    keys = dot_nt(y, w_t[width:2 * width, :]).astype(BF16)
    values = dot_nt(w_t[2 * width:3 * width, :], y).astype(BF16)
    gate = sigmoid(dot_nt(w_t[3 * width:4 * width, :], y))
    zeros = jnp.zeros((2 * HD, two), BF16)
    pieces = []
    for pair in range(width // (2 * HD)):
        rows = q2[2 * HD * pair:2 * HD * (pair + 1), :]
        lanes = 128 * (pair // 2)
        stacked = jnp.concatenate([rows, zeros] if pair % 2 == 0 else [zeros, rows], axis=0)
        logits = dot(keys[:, lanes:lanes + 128], stacked)
        probs = softmax_cols(logits * scale + bias_of(pair))
        mixed = dot(values[2 * HD * pair:2 * HD * (pair + 1), :], probs)
        pieces.append(mixed[0:HD, 0:length])
        pieces.append(mixed[HD:2 * HD, length:two])
    gated = (gate * jnp.concatenate(pieces, axis=0)).astype(BF16)
    return dot_tn(gated, w_out[...])


def column_attention(y, w_t, w_out, mask_bias):
    length, width = y.shape
    heads = width // HD
    scale = HD ** -0.5 * LOG2E
    wide = heads * length
    q_all = dot_nt(w_t[0:width, :], jnp.concatenate([y] * heads, axis=0))
    q_all = jnp.where(iota((width, wide), 0) // HD == iota((width, wide), 1) // length, q_all, 0.0).astype(BF16)
    keys = dot_nt(y, w_t[width:2 * width, :]).astype(BF16)
    values = dot_nt(w_t[2 * width:3 * width, :], y).astype(BF16)
    gate = sigmoid(dot_nt(w_t[3 * width:4 * width, :], y))
    probs = softmax_cols(dot(keys, q_all) * scale + mask_bias)
    mixed = dot(values, probs)
    pieces = [mixed[HD * h:HD * (h + 1), length * h:length * (h + 1)] for h in range(heads)]
    gated = (gate * jnp.concatenate(pieces, axis=0)).astype(BF16)
    return dot_tn(gated, w_out[...])


def block_kernel(n, x_ref, z_ref, mm_ref, rm_ref,
                 w_rb, w_r, w_ro, w_c, w_co, w_ac, w_oo, w_tsb, w_ts, w_tso, w_teb, w_te, w_teo,
                 p2, p2t, p3, p3t, p4, p4e, p5, p6, eye, tok,
                 out_m, out_z,
                 g_row, g_c, g_t1, g_t2, s1, r1, s2, r2, s3, r3, s4, r4,
                 tmp_b, b_q, bm_row, bm_tri, x1, y1, m_t, rn, a_t, c_t, c_f, u_s, w_f32, w_fe, z1, yn, x3,
                 gs_a, gr_a, gs_b, gr_b, as_sem, ar_sem):
    me = lax.axis_index(GROUP_AXIS)
    chips = n // 2
    chip = me // 2
    core = me % 2
    partner = me + 1 - 2 * core
    crops, seqs, length, width = x_ref.shape
    rows = z_ref.shape[1]
    quads = rows // 4
    blocks = length // 64
    blk = 4 * rows
    sup = 4 * blk
    steps = []
    for k in range(1, chips // 2 + 1):
        steps.append(k)
        if chips - k != k:
            steps.append(chips - k)

    barrier = pltpu.get_barrier_semaphore()
    for k in range(1, n):
        pl.semaphore_signal(barrier, inc=1, device_id={GROUP_AXIS: lax.rem(me + k, n)}, device_id_type=MESH)
    pl.semaphore_wait(barrier, n - 1)

    def remote(src, dst, send, recv, device):
        return pltpu.make_async_remote_copy(src_ref=src, dst_ref=dst, send_sem=send, recv_sem=recv,
                                            device_id={GROUP_AXIS: device}, device_id_type=MESH)

    def same_core(k):
        return 2 * lax.rem(chip + k, chips) + core

    def gather_start(buf, e, c):
        mine = buf.at[c, me]
        for k in steps:
            remote(mine, mine, gs_a.at[e, c], gr_a.at[e, c], same_core(k)).start()
        remote(mine, mine, gs_b.at[e, c], gr_b.at[e, c], partner).start()

    def wait_bytes(ref, sem):
        pltpu.make_async_copy(ref, ref, sem).wait()

    def gather_forward(buf, e, c):
        wait_bytes(buf.at[c, pl.ds(0, chips - 1)], gr_a.at[e, c])
        for k in steps:
            block = buf.at[c, same_core(k)]
            remote(block, block, gs_b.at[e, c], gr_b.at[e, c], partner).start()

    def gather_wait(buf, e, c):
        wait_bytes(buf.at[c, pl.ds(0, chips)], gr_b.at[e, c])

    def gather_end(buf, e, c):
        wait_bytes(buf.at[c, pl.ds(0, chips - 1)], gs_a.at[e, c])
        wait_bytes(buf.at[c, pl.ds(0, chips)], gs_b.at[e, c])

    def block_of(ref, c, d, planes):
        where = pl.ds(pl.multiple_of(d * blk, 16), blk)
        return ref.at[c, :, where, :] if planes else ref.at[c, where, :]

    def exchange_start(src, dst, e, c, planes):
        here = pl.ds(pl.multiple_of(me * blk, 16), blk)
        if planes:
            dst[c, :, here, :] = src[c, :, here, :]
        else:
            dst[c, here, :] = src[c, here, :]
        landing = block_of(dst, c, me, planes)
        for k in steps:
            for other in range(2):
                d = 2 * lax.rem(chip + k, chips) + (core + other) % 2
                remote(block_of(src, c, d, planes), landing, as_sem.at[e, c], ar_sem.at[e, c], d).start()
        remote(block_of(src, c, partner, planes), landing, as_sem.at[e, c], ar_sem.at[e, c], partner).start()

    def others(ref, c, planes):
        where = pl.ds(0, (n - 1) * blk)
        return ref.at[c, :, where, :] if planes else ref.at[c, where, :]

    def exchange_wait(dst, e, c, planes):
        wait_bytes(others(dst, c, planes), ar_sem.at[e, c])

    def exchange_end(src, e, c, planes):
        wait_bytes(others(src, c, planes), as_sem.at[e, c])

    def loop(count, body):
        lax.fori_loop(0, count, lambda i, carry: (body(i), carry)[1], 0)

    tmp_b[...] = jnp.zeros_like(tmp_b)

    def row_bias(c):
        def one(i):
            tmp_b[pl.ds(pl.multiple_of(i * 8, 8), 8), :] = dot_nt(w_rb[...], layer_norm(z_ref[c, i]))
        loop(rows, one)
        g_row[c, me] = dot(p6[...], tmp_b[...].astype(BF16)).astype(BF16)
        gather_start(g_row, 0, c)
    loop(crops, row_bias)

    w_f32[...] = w_oo[...].astype(F32)
    for fp in range(HD // 2):
        for half in range(2):
            at = fp * 2 * HD + half * HD
            w_fe[at:at + HD, :] = w_f32[pl.ds(half * (HD // 2) + fp, HD, stride=HD), :].astype(BF16)

    def unpack_bias(buf, c, group, perm, first, pieces, piece):
        for sb in range(n // 4):
            part = buf[c, 4 * sb:4 * sb + 4, blk * group:blk * (group + 1), :]
            moved = dot(perm[...], part.reshape(sup, length)).astype(BF16)
            for i in range(pieces):
                at = first + i * (length * 4 // pieces) + sb * piece
                b_q[at:at + piece, :] = moved[i * piece:(i + 1) * piece, :]

    def mask_columns(row, select):
        wide = jnp.broadcast_to(row.astype(F32), (128, length)).astype(BF16)
        return (dot_nt(select[...], wide) - 1.0) * (MASK_SCALE * LOG2E)

    def row_attention(c):
        gather_forward(g_row, 0, c)
        gather_wait(g_row, 0, c)
        for group in range(width // HD // 4):
            unpack_bias(g_row, c, group, p4, group * 4 * length, 4, blk)
        for pair in range(width // HD // 2):
            at = 2 * length * pair
            bm_row[:, at:at + 2 * length] = dot_nt(eye[...], b_q[at:at + 2 * length, :]) * LOG2E

        def one(s):
            x = x_ref[c, s]
            col = mask_columns(mm_ref[c, pl.ds(me * seqs + s, 1), :], eye)
            col3 = jnp.concatenate([col] * (2 * length // 128), axis=1)
            update = pair_attention(layer_norm(x), w_r, w_ro,
                                    lambda pair: bm_row[:, 2 * length * pair:2 * length * (pair + 1)] + col3)
            x1[s] = (x.astype(F32) + update).astype(BF16)
        loop(seqs, one)
        for b in range(blocks):
            part = x1[:, 64 * b:64 * (b + 1), :].reshape(256, width)
            s1[c, 256 * b:256 * (b + 1), :] = dot(p2[...], part).astype(BF16)
        exchange_start(s1, r1, 0, c, False)
    loop(crops, row_attention)

    def columns(c):
        exchange_wait(r1, 0, c, False)
        for sb in range(n // 4):
            moved = dot(p3[...], r1[c, sup * sb:sup * (sb + 1), :]).astype(BF16)
            for i in range(rows):
                y1[i, 16 * sb:16 * (sb + 1), :] = moved[16 * i:16 * (i + 1), :]
        n_seq = y1.shape[1]
        mk = mm_ref[c].astype(F32).astype(BF16)
        mine = (iota((16, length), 1) == me * rows + iota((16, length), 0)).astype(F32).astype(BF16)
        m_t[...] = dot_nt(mine, jnp.concatenate([mk, mk], axis=0))
        rn[c] = 1.0 / (dot(m_t[:, 0:n_seq].astype(BF16), mk) + OPM_EPS)
        low = iota((HD, 2 * n_seq), 1) < n_seq

        def one(i):
            x = y1[i]
            pick = (iota((128, length), 1) == me * rows + i).astype(F32).astype(BF16)
            col = (dot_nt(mk, pick) - 1.0) * (MASK_SCALE * LOG2E)
            heads = width // HD
            update = column_attention(layer_norm(x), w_c, w_co, jnp.concatenate([col] * (heads * n_seq // 128), axis=1))
            x = (x.astype(F32) + update).astype(BF16)
            y1[i] = x
            y = layer_norm(x)
            both = dot_nt(w_ac[...], jnp.concatenate([y, y], axis=0)).astype(BF16).astype(F32)
            both = both * m_t[pl.ds(i, 1), :]
            a = both[0:HD, :]
            at = pl.ds(pl.multiple_of(i * HD, HD), HD)
            a_t[c, 0, at, :] = jnp.where(low, a, 0.0).astype(BF16)
            a_t[c, 1, at, :] = jnp.where(low, 0.0, a).astype(BF16)
            half = HD // 2
            packed = jnp.where(low[0:half], both[HD:HD + half, :], both[HD + half:2 * HD, :])
            c_t[pl.ds(pl.multiple_of(i * half, half), half), :] = packed.astype(BF16)
        loop(rows, one)
        g_c[c, me] = dot(p5[...], c_t[...]).astype(BF16)
        gather_start(g_c, 1, c)
        for db in range(n // 4):
            part = y1[:, 16 * db:16 * (db + 1), :].reshape(16 * rows, width)
            s2[c, sup * db:sup * (db + 1), :] = dot(p3t[...], part).astype(BF16)
        exchange_start(s2, r2, 1, c, False)
    loop(crops, columns)

    def bias_send(buf, e, c):
        buf[c, me] = dot(p6[0:blk, :], tmp_b[...].astype(BF16)).astype(BF16)
        gather_start(buf, e, c)

    def outer(c):
        gather_forward(g_c, 1, c)
        gather_wait(g_c, 1, c)

        def unpack(q):
            for sb in range(n // 4):
                part = g_c[c, 4 * sb:4 * sb + 4, pl.ds(pl.multiple_of(blk * q, 16), blk), :].reshape(sup, 128)
                moved = dot(p4[...], part).astype(BF16)
                for i in range(4):
                    c_f[4 * q + i, blk * sb:blk * (sb + 1), :] = moved[blk * i:blk * (i + 1), :]
        loop(HD // 2 // 4, unpack)

        def products(fp):
            for half in range(2):
                u = dot_nt(a_t[c, half], c_f[fp])
                for i in range(rows):
                    at = pl.ds(pl.multiple_of(fp * 2 * HD + half * HD, HD), HD)
                    u_s[i, at, :] = (u[HD * i:HD * (i + 1), :] * rn[c, i:i + 1, :]).astype(BF16)
        loop(HD // 2, products)

        def one(i):
            update = dot_tn(u_s[i], w_fe[...])
            z = (z_ref[c, i].astype(F32) + update).astype(BF16)
            z1[c, i] = z
            y = layer_norm(z)
            yn[c, i] = y
            tmp_b[pl.ds(pl.multiple_of(i * 8, 8), 4), :] = dot_nt(w_tsb[...], y)
        loop(rows, one)
        bias_send(g_t1, 2, c)
    loop(crops, outer)

    def triangle(buf, e, c, perm, pieces, piece, select, w_t, w_out):
        gather_forward(buf, e, c)
        gather_wait(buf, e, c)
        unpack_bias(buf, c, 0, perm, 0, pieces, piece)
        col = mask_columns(rm_ref[c], select)
        col3 = jnp.concatenate([col] * (2 * length // 128), axis=1)
        for pair in range(2):
            at = 2 * length * pair
            bm_tri[:, at:at + 2 * length] = dot_nt(eye[...], b_q[at:at + 2 * length, :]) * LOG2E + col3

        def one(i):
            update = pair_attention(yn[c, i], w_t, w_out,
                                    lambda pair: bm_tri[:, 2 * length * pair:2 * length * (pair + 1)])
            x3[i] = (z1[c, i].astype(F32) + update).astype(BF16)
        loop(rows, one)

    def start_node(c):
        triangle(g_t1, 2, c, p4, 4, blk, eye, w_ts, w_tso)
        for q in range(quads):
            for b in range(blocks):
                part = x3[4 * q:4 * q + 4, 64 * b:64 * (b + 1), :].reshape(256, 128)
                s3[c, q, 256 * b:256 * (b + 1), :] = dot(p2[...], part).astype(BF16)
        exchange_start(s3, r3, 2, c, True)
    loop(crops, start_node)

    def transposed(c):
        exchange_wait(r3, 2, c, True)
        for q in range(quads):
            for sb in range(n // 4):
                moved = dot(p3[...], r3[c, q, sup * sb:sup * (sb + 1), :]).astype(BF16)
                for i in range(rows):
                    at = 64 * q + 16 * sb
                    z1[c, i, at:at + 16, :] = moved[16 * i:16 * (i + 1), :]

        def one(i):
            y = layer_norm(z1[c, i])
            yn[c, i] = y
            tmp_b[pl.ds(pl.multiple_of(i * 8, 8), 4), :] = dot_nt(w_teb[...], y)
        loop(rows, one)
        bias_send(g_t2, 3, c)
    loop(crops, transposed)

    def end_node(c):
        triangle(g_t2, 3, c, p4e, 4 * quads, 16, tok, w_te, w_teo)
        for q in range(quads):
            for db in range(n // 4):
                part = x3[:, 64 * q + 16 * db:64 * q + 16 * (db + 1), :].reshape(16 * rows, 128)
                s4[c, q, sup * db:sup * (db + 1), :] = dot(p3t[...], part).astype(BF16)
        exchange_start(s4, r4, 3, c, True)
    loop(crops, end_node)

    def finish(c):
        exchange_wait(r2, 1, c, False)
        for b in range(blocks):
            moved = dot(p2t[...], r2[c, 256 * b:256 * (b + 1), :]).astype(BF16)
            for i in range(seqs):
                out_m[c, i, 64 * b:64 * (b + 1), :] = moved[64 * i:64 * (i + 1), :]
        exchange_wait(r4, 3, c, True)
        for q in range(quads):
            for b in range(blocks):
                moved = dot(p2t[...], r4[c, q, 256 * b:256 * (b + 1), :]).astype(BF16)
                for i in range(4):
                    out_z[c, 4 * q + i, 64 * b:64 * (b + 1), :] = moved[64 * i:64 * (i + 1), :]
    loop(crops, finish)

    def drain(c):
        for e, buf in enumerate((g_row, g_c, g_t1, g_t2)):
            gather_end(buf, e, c)
        for e, (buf, planes) in enumerate(((s1, False), (s2, False), (s3, True), (s4, True))):
            exchange_end(buf, e, c, planes)
    loop(crops, drain)


def solution(mesh):
    n = mesh.shape[GROUP_AXIS]
    rows_spec = P(PART_AXIS, GROUP_AXIS, None, None)
    in_specs = (rows_spec, rows_spec, P(PART_AXIS, None, None), P(PART_AXIS, None)) + (P(),) * N_WEIGHTS

    def local_block(msa, pair, msa_mask, res_mask, *weights):
        (w_rb, w_r, w_ro, w_c, w_co, w_ac, w_oo, w_tsb, w_ts, w_tso, w_teb, w_te, w_teo) = weights
        crops, seqs, length, width = msa.shape
        rows, pair_width = pair.shape[1], pair.shape[3]
        n_seq = msa_mask.shape[1]
        heads, tri_heads = w_r.shape[2], w_ts.shape[2]
        quads = rows // 4

        def flat_t(w):
            return jnp.transpose(w, (1, 2, 3, 0)).reshape(-1, w.shape[0])

        operands = [
            msa, pair, msa_mask, res_mask.reshape(crops, 1, length),
            w_rb.T, flat_t(w_r), w_ro.reshape(width, width), flat_t(w_c), w_co.reshape(width, width),
            jnp.transpose(w_ac, (1, 2, 0)).reshape(-1, width), w_oo.reshape(-1, pair_width),
            w_tsb.T, flat_t(w_ts), w_tso.reshape(pair_width, pair_width),
            w_teb.T, flat_t(w_te), w_teo.reshape(pair_width, pair_width),
        ]
        p2 = permutation((4, 64), (1, 0))
        p3 = permutation((4, rows, 4), (1, 0, 2))
        p4 = permutation((4, 4, rows), (1, 0, 2))
        p4e = permutation((4, 4, quads, 4), (1, 2, 0, 3))
        p5 = permutation((rows, HD // 2), (1, 0))
        p6 = permutation((rows, heads), (1, 0))
        tok = permutation((n, quads, 4), (1, 0, 2))
        consts = [p2, p2.T, p3, p3.T, p4, p4e, p5, p6, np.eye(length), tok]
        operands += [jnp.asarray(a, BF16) for a in consts]

        vmem = pl.BlockSpec(memory_space=pltpu.VMEM)
        total = n * 4 * rows
        scratch = [
            pltpu.VMEM((crops, n, heads * rows, length), BF16),
            pltpu.VMEM((crops, n, HD // 2 * rows, 128), BF16),
            pltpu.VMEM((crops, n, tri_heads * rows, length), BF16),
            pltpu.VMEM((crops, n, tri_heads * rows, length), BF16),
        ]
        scratch += [pltpu.VMEM((crops, total, width), BF16)] * 4
        scratch += [pltpu.VMEM((crops, quads, total, pair_width), BF16)] * 4
        scratch += [
            pltpu.VMEM((8 * rows, length), F32),
            pltpu.VMEM((heads * length, length), BF16),
            pltpu.VMEM((length, heads * length), F32),
            pltpu.VMEM((length, tri_heads * length), F32),
            pltpu.VMEM((seqs, length, width), BF16),
            pltpu.VMEM((rows, n_seq, width), BF16),
            pltpu.VMEM((16, 2 * n_seq), F32),
            pltpu.VMEM((crops, 16, length), F32),
            pltpu.VMEM((crops, 2, rows * HD, 128), BF16),
            pltpu.VMEM((rows * HD // 2, 128), BF16),
            pltpu.VMEM((HD // 2, length, 128), BF16),
            pltpu.VMEM((rows, HD * HD, length), BF16),
            pltpu.VMEM((HD * HD, pair_width), F32),
            pltpu.VMEM((HD * HD, pair_width), BF16),
            pltpu.VMEM((crops, rows, length, pair_width), BF16),
            pltpu.VMEM((crops, rows, length, pair_width), BF16),
            pltpu.VMEM((rows, length, pair_width), BF16),
        ]
        scratch += [pltpu.SemaphoreType.DMA((4, crops))] * 6
        return pl.pallas_call(
            functools.partial(block_kernel, n),
            out_shape=(jax.ShapeDtypeStruct(msa.shape, BF16), jax.ShapeDtypeStruct(pair.shape, BF16)),
            in_specs=[vmem] * len(operands),
            out_specs=(vmem, vmem),
            scratch_shapes=scratch,
            compiler_params=pltpu.CompilerParams(collective_id=0, has_side_effects=True, vmem_limit_bytes=VMEM_BYTES),
            name='evoformer_block',
        )(*operands)

    return jax.shard_map(local_block, mesh=mesh, in_specs=in_specs, out_specs=(rows_spec, rows_spec),
                         check_vma=False)
```

time: 488 us -> 226 us (0.46); the launches traced: 480 us -> 223 us
  Pallas kernels: 0 us -> 218 us
  blocking collectives: 183 us -> 0 us
  matrix products: 143 us -> 0 us
  waiting for transfers between devices: 48.6 us -> 0 us
  starting transfers between devices: 40.6 us -> 0 us
  local copies, waits for them, and re-layouts: 36.9 us -> 4.44 us
  other arithmetic: 26.3 us -> 0 us
    pallas_call x0 -> x1, Pallas kernels: none -> 218 us  [local_block(): pl.pallas_call(functools.partial(block_kernel, n), out_shape=(jax.ShapeDt...]
    all_gather x8 -> x0, blocking collectives: 183 us -> none  [the longest x6 142 us: gathered_bias(): return lax.all_gather(bias_part, GROUP_AXIS, axis=1, tiled=True)]
    dot_general x30 -> x0, matrix products: 92 us -> none  [the longest x8 39.9 us: gated_attention(): jnp.einsum('qhd,hdc->qc', mixed.astype(jnp.bfloat16), w_out, preferred_el...]
    sub x6 -> x0, matrix products: 50.6 us -> none  [gated_attention(): attn_prob = jax.nn.softmax(logits, axis=-1).astype(jnp.bfloat16)]
    all_to_all x8 -> x0, waiting for transfers between devices: 48.6 us -> none  [the longest x2 31.6 us: crop_block(): lax.all_to_all(jnp.swapaxes(pair_cols, 0, 1), GROUP_AXIS, 0, 1, tiled=True)]
    all_to_all x8 -> x0, starting transfers between devices: 40.6 us -> none  [the longest x2 11.9 us: crop_block(): lax.all_to_all(value_a8, GROUP_AXIS, 1, 0, tiled=True)]
    convert_element_type x26 -> x0, local copies, waits for them, and re-layouts: 30.5 us -> none  [the longest x18 23.7 us: gated_attention(): return (x_row.astype(jnp.float32) + update).astype(jnp.bfloat16)]
    reduce_sum x16 -> x0, other arithmetic: 13.7 us -> none  [the longest x10 9.01 us: layer_norm(): var_val = jnp.mean(centred * centred, axis=-1, keepdims=True)]
  transfers between devices with their start and end apart: 8 -> 0, of which waited for: 4 -> 0; matrix products, arithmetic and copies ran while one was open for 22% -> 0% of each run, Pallas kernels for 0% -> 0%
where the time goes in v1:
time: 226 us; the launch traced here: 223 us
  Pallas kernels  218 us (96%)
  local copies, waits for them, and re-layouts  4.44 us (2%)
    pallas_call x1, Pallas kernels, local_block(): pl.pallas_call(functools.partial(block_kernel, n), out_shape=(jax.ShapeDt...  218 us

profile of v1, /device:TPU:21, one launch (start us, length us, event | category | flops | bytes accessed | tf_op | source)
XLA Modules:
  0.0 223.4 jit_solution(15105595607500652003)
XLA Ops:
  0.6 1.3 reshape.37.rm_ref
  1.9 218.3 %evoformer_block.1 = (bf16[2,4,192,256]{3,2,1,0:T(8,128)(2,1)}, bf16[2,12,192,128]{3,2,1,0:T(8,128)(2,1)}) custom-call(bf16[2,4,192,256]{3,2,1,0:T(8,128)(2,1)} %x_ref.1, bf16[2,12,192,128]{3,2,1,0:T(8,128)(2,1)} %z_ref.1, s32[2,64,192]{2,1,0:T(8,128)} %mm_ref.1, s32[2,1,192]{2,1,0:T(1,128)} %reshape.37.rm_ref, bf16[8,128]{1,0:T(8,128)(2,1)} %bitcast.33, ...), custom_call_target="tpu_custom_call" | custom-call | tf_op jit(solution)/shard_map/evoformer_block/pallas_call | solution.py:460
  220.2 0.0 copy-start
  220.2 2.2 copy.31
  222.4 0.0 copy-done
  222.4 1.0 copy.32
Async XLA Ops:
  220.2 2.2 copy-start

commit v2 on v1

v2 whole, which is shorter than its diff:
```python
import functools
import math

import jax
import jax.numpy as jnp
import numpy as np
from jax import lax
from jax.experimental import pallas as pl
from jax.experimental.pallas import tpu as pltpu
from jax.sharding import PartitionSpec as P

MASK_SCALE = 10000.0
LN_EPS = 1e-5
OPM_EPS = 1e-3
LOG2E = math.log2(math.e)
N_WEIGHTS = 13
PART_AXIS = 'data'
GROUP_AXIS = 'dap'
MESH = pl.DeviceIdType.MESH
F32 = jnp.float32
BF16 = jnp.bfloat16
HD = 32
U_LN, U_UNP, U_PROD, U_OUT = 12, 2, 4, 3
U_PR, U_PO, U_TP, U_TA, U_CP, U_CM, U_CA, U_CF = 2, 4, 3, 4, 1, 1, 3, 3
VMEM_BYTES = 60 * 1024 * 1024


def dot(a, b):
    return lax.dot_general(a, b, (((1,), (0,)), ((), ())), preferred_element_type=F32)


def dot_nt(a, b):
    return lax.dot_general(a, b, (((1,), (1,)), ((), ())), preferred_element_type=F32)


def dot_tn(a, b):
    return lax.dot_general(a, b, (((0,), (0,)), ((), ())), preferred_element_type=F32)


def layer_norm(x):
    x_float = x.astype(F32)
    centred = x_float - jnp.mean(x_float, axis=-1, keepdims=True)
    var = jnp.mean(centred * centred, axis=-1, keepdims=True)
    return (centred * lax.rsqrt(var + LN_EPS)).astype(BF16)


def seg(i, size):
    return slice(i * size, (i + 1) * size)


def sigmoid(x):
    return 1.0 / (1.0 + jnp.exp2(x * (-LOG2E)))


def iota(shape, dim):
    return lax.broadcasted_iota(jnp.int32, shape, dim)


def permutation(sizes, order, keep=None):
    total = int(np.prod(sizes))
    source = np.arange(total).reshape(sizes).transpose(order).reshape(-1)
    out = np.zeros((total, total), np.float32)
    out[np.arange(total), source] = 1.0
    return out


def softmax_cols(t):
    e = jnp.exp2(t - jnp.max(t, axis=0, keepdims=True))
    return (e * (1.0 / jnp.sum(e, axis=0, keepdims=True))).astype(BF16)


def same_half(width, lanes, half):
    return (iota((width, lanes), 0) // HD) % 2 == (iota((width, lanes), 1) // half) % 2


def block_kernel(n, x_ref, z_ref, mm_ref, rm_ref,
                 w_rb, w_r, w_ro, w_c, w_co, w_ac, w_oo, w_tsb, w_ts, w_tso, w_teb, w_te, w_teo,
                 p2, p2t, p3, p3t, p4, p4e, p5, p6, eye, tok,
                 out_m, out_z,
                 g_row, g_c, g_t1, g_t2, s1, r1, s2, r2, s3, r3, s4, r4,
                 tmp_b, b_q, bm_row, bm_tri, x1, y1, m_t, rn, a_t, c_t, c_f, u_s, w_f32, w_fe, w_fet, z1, yn, x3,
                 q_s, k_s, v_s, g_s, o_s, s_buf, m_s, qc_s, kc_s, vc_s, gc_s, oc_s, mc_s,
                 gs_a, gr_a, gs_b, gr_b, as_sem, ar_sem):
    me = lax.axis_index(GROUP_AXIS)
    chips = n // 2
    chip = me // 2
    core = me % 2
    partner = me + 1 - 2 * core
    crops, seqs, length, width = x_ref.shape
    rows = z_ref.shape[1]
    quads = rows // 4
    blocks = length // 64
    blk = 4 * rows
    sup = 4 * blk
    steps = []
    for k in range(1, chips // 2 + 1):
        steps.append(k)
        if chips - k != k:
            steps.append(chips - k)

    barrier = pltpu.get_barrier_semaphore()
    for k in range(1, n):
        pl.semaphore_signal(barrier, inc=1, device_id={GROUP_AXIS: lax.rem(me + k, n)}, device_id_type=MESH)
    pl.semaphore_wait(barrier, n - 1)

    def remote(src, dst, send, recv, device):
        return pltpu.make_async_remote_copy(src_ref=src, dst_ref=dst, send_sem=send, recv_sem=recv,
                                            device_id={GROUP_AXIS: device}, device_id_type=MESH)

    def same_core(k):
        return 2 * lax.rem(chip + k, chips) + core

    def gather_start(buf, e, c):
        mine = buf.at[c, me]
        for k in steps:
            remote(mine, mine, gs_a.at[e, c], gr_a.at[e, c], same_core(k)).start()
        remote(mine, mine, gs_b.at[e, c], gr_b.at[e, c], partner).start()

    def wait_bytes(ref, sem):
        pltpu.make_async_copy(ref, ref, sem).wait()

    def gather_forward(buf, e, c):
        wait_bytes(buf.at[c, pl.ds(0, chips - 1)], gr_a.at[e, c])
        for k in steps:
            block = buf.at[c, same_core(k)]
            remote(block, block, gs_b.at[e, c], gr_b.at[e, c], partner).start()

    def gather_wait(buf, e, c):
        wait_bytes(buf.at[c, pl.ds(0, chips)], gr_b.at[e, c])

    def gather_end(buf, e, c):
        wait_bytes(buf.at[c, pl.ds(0, chips - 1)], gs_a.at[e, c])
        wait_bytes(buf.at[c, pl.ds(0, chips)], gs_b.at[e, c])

    def block_of(ref, c, d, planes):
        where = pl.ds(pl.multiple_of(d * blk, 16), blk)
        return ref.at[c, :, where, :] if planes else ref.at[c, where, :]

    def exchange_start(src, dst, e, c, planes):
        here = pl.ds(pl.multiple_of(me * blk, 16), blk)
        if planes:
            dst[c, :, here, :] = src[c, :, here, :]
        else:
            dst[c, here, :] = src[c, here, :]
        landing = block_of(dst, c, me, planes)
        for k in steps:
            for other in range(2):
                d = 2 * lax.rem(chip + k, chips) + (core + other) % 2
                remote(block_of(src, c, d, planes), landing, as_sem.at[e, c], ar_sem.at[e, c], d).start()
        remote(block_of(src, c, partner, planes), landing, as_sem.at[e, c], ar_sem.at[e, c], partner).start()

    def others(ref, c, planes):
        where = pl.ds(0, (n - 1) * blk)
        return ref.at[c, :, where, :] if planes else ref.at[c, where, :]

    def exchange_wait(dst, e, c, planes):
        wait_bytes(others(dst, c, planes), ar_sem.at[e, c])

    def exchange_end(src, e, c, planes):
        wait_bytes(others(src, c, planes), as_sem.at[e, c])

    def loop(count, body, unroll=1):
        def several(i, carry):
            for k in range(unroll):
                body(i * unroll + k)
            return carry
        lax.fori_loop(0, count // unroll, several, 0)

    tmp_b[:] = jnp.zeros_like(tmp_b)

    def row_bias(c):
        def one(i):
            tmp_b[pl.ds(pl.multiple_of(i * 8, 8), 8), :] = dot_nt(w_rb[:], layer_norm(z_ref[c, i]))
        loop(rows, one, U_LN)
        g_row[c, me] = dot(p6[:], tmp_b[:].astype(BF16)).astype(BF16)
        gather_start(g_row, 0, c)
    loop(crops, row_bias)

    w_f32[:] = w_oo[:].astype(F32)
    for fp in range(HD // 2):
        for half in range(2):
            at = fp * 2 * HD + half * HD
            w_fe[at:at + HD, :] = w_f32[pl.ds(half * (HD // 2) + fp, HD, stride=HD), :]
    for b in range(HD * HD // 128):
        w_fet[:, seg(b, 128)] = w_fe[seg(b, 128), :].T.astype(BF16)
    q_s[:] = jnp.zeros_like(q_s)

    def unpack_bias(buf, c, group, perm, first, pieces, piece):
        for sb in range(n // 4):
            part = buf[c, 4 * sb:4 * sb + 4, seg(group, blk), :]
            moved = dot(perm[:], part.reshape(sup, length)).astype(BF16)
            for i in range(pieces):
                at = first + i * (length * 4 // pieces) + sb * piece
                b_q[at:at + piece, :] = moved[i * piece:(i + 1) * piece, :]

    def mask_columns(row, select):
        wide = jnp.broadcast_to(row.astype(F32), (128, length)).astype(BF16)
        return (dot_nt(select[:], wide) - 1.0) * (MASK_SCALE * LOG2E)

    scale = HD ** -0.5 * LOG2E
    two, four = 2 * length, 4 * length

    def project(y, w_t, first):
        wide = y.shape[1]
        q = dot_nt(w_t[0:wide, :], jnp.concatenate([y, y], axis=0))
        q = jnp.where(same_half(wide, two, length), q, 0.0).astype(BF16)
        keys = dot_nt(y, w_t[wide:2 * wide, :]).astype(BF16)
        values = dot_nt(w_t[2 * wide:3 * wide, :], y).astype(BF16)
        gate = sigmoid(dot_nt(w_t[3 * wide:4 * wide, :], y))
        for g in range(wide // 128):
            u = first + g
            q_s[u, 0:64, 0:two] = q[128 * g:128 * g + 64, :]
            q_s[u, 64:128, two:four] = q[128 * g + 64:128 * g + 128, :]
            k_s[u] = keys[:, seg(g, 128)]
            v_s[u] = values[seg(g, 128), :]
            g_s[u] = gate[seg(g, 128), :]

    def attend(count, bias_of):
        def mix(u, probs):
            pieces = []
            for p in range(2):
                mixed = dot(v_s[u, seg(p, 64), :], probs[:, seg(p, two)])
                pieces += [mixed[0:HD, 0:length], mixed[HD:2 * HD, length:two]]
            return jnp.concatenate(pieces, axis=0)

        def finish(u, mixed):
            o_s[u] = (g_s[u] * mixed).astype(BF16)

        s_buf[0] = dot(k_s[0], q_s[0])

        def pair(i):
            u = 2 * i
            s_buf[1] = dot(k_s[u + 1], q_s[u + 1])
            mixed = mix(u, softmax_cols(s_buf[0] * scale + bias_of(u)))
            after = jnp.minimum(u + 2, count - 1)
            s_buf[0] = dot(k_s[after], q_s[after])
            probs = softmax_cols(s_buf[1] * scale + bias_of(u + 1))
            finish(u, mixed)
            finish(u + 1, mix(u + 1, probs))
        loop(count // 2, pair)

    groups = width // 128

    def row_attention(c):
        gather_forward(g_row, 0, c)
        gather_wait(g_row, 0, c)
        for group in range(groups):
            unpack_bias(g_row, c, group, p4, group * four, 4, blk)
        for pair in range(2 * groups):
            bm_row[pair // 2, :, two * (pair % 2):two * (pair % 2 + 1)] = \
                dot_nt(eye[:], b_q[seg(pair, two), :]) * LOG2E

        def before(s):
            m_s[s] = mask_columns(mm_ref[c, pl.ds(me * seqs + s, 1), :], eye)
            project(layer_norm(x_ref[c, s]), w_r, s * groups)
        loop(seqs, before, U_PR)

        def bias_of(u):
            return bm_row[u % groups] + jnp.concatenate([m_s[u // groups]] * (four // 128), axis=1)
        attend(seqs * groups, bias_of)

        def after(s):
            gated = jnp.concatenate([o_s[s * groups + g] for g in range(groups)], axis=0)
            x1[s] = (x_ref[c, s].astype(F32) + dot_tn(gated, w_ro[:])).astype(BF16)
        loop(seqs, after, U_PO)
        for b in range(blocks):
            part = x1[:, seg(b, 64), :].reshape(256, width)
            s1[c, seg(b, 256), :] = dot(p2[:], part).astype(BF16)
        exchange_start(s1, r1, 0, c, False)
    loop(crops, row_attention)

    def columns(c):
        exchange_wait(r1, 0, c, False)
        for sb in range(n // 4):
            moved = dot(p3[:], r1[c, seg(sb, sup), :]).astype(BF16)
            for i in range(rows):
                y1[i, seg(sb, 16), :] = moved[seg(i, 16), :]
        n_seq = y1.shape[1]
        mk = mm_ref[c].astype(F32).astype(BF16)
        mine = (iota((16, length), 1) == me * rows + iota((16, length), 0)).astype(F32).astype(BF16)
        m_t[:] = dot_nt(mine, jnp.concatenate([mk, mk], axis=0))
        rn[c] = 1.0 / (dot(m_t[:, 0:n_seq].astype(BF16), mk) + OPM_EPS)
        low = iota((HD, 2 * n_seq), 1) < n_seq
        picks = (iota((128 * rows, length), 1) == me * rows + iota((128 * rows, length), 0) // 128)
        mask_all = (dot_nt(mk, picks.astype(F32).astype(BF16)) - 1.0) * (MASK_SCALE * LOG2E)
        for i in range(rows):
            mc_s[i] = mask_all[:, seg(i, 128)]
        tokens = 4 * n_seq

        def doubled(y):
            return jnp.concatenate([y[n_seq * (r // 2):n_seq * (r // 2 + 1), :] for r in range(8)], axis=0)

        def before(q):
            y = layer_norm(y1[pl.ds(4 * q, 4)].reshape(tokens, width))
            qq = dot_nt(w_c[0:width, :], doubled(y))
            qc_s[q] = jnp.where(same_half(width, 2 * tokens, n_seq), qq, 0.0).astype(BF16)
            kc_s[q] = dot_nt(y, w_c[width:2 * width, :]).astype(BF16)
            vc_s[q] = dot_nt(y, w_c[2 * width:3 * width, :]).astype(BF16)
            gc_s[q] = sigmoid(dot_nt(w_c[3 * width:4 * width, :], y))
        loop(quads, before, U_CP)

        def middle(q):
            zeros = jnp.zeros((64, 128), BF16)
            for g in range(groups):
                heads = [[] for _ in range(4)]
                for r in range(4):
                    at = n_seq * r
                    wide = qc_s[q, seg(g, 128), seg(r, 128)]
                    stacked = jnp.concatenate([jnp.concatenate([wide[0:64], zeros], axis=0),
                                               jnp.concatenate([zeros, wide[64:128]], axis=0)], axis=1)
                    logits = dot(kc_s[q, at:at + n_seq, seg(g, 128)], stacked)
                    col = mc_s[4 * q + r]
                    probs = softmax_cols(logits * scale + jnp.concatenate([col, col], axis=1))
                    mixed = dot_tn(vc_s[q, at:at + n_seq, seg(g, 128)], probs)
                    for h in range(4):
                        heads[h].append(mixed[seg(h, HD), seg(h, n_seq)])
                mixed = jnp.concatenate([jnp.concatenate(h, axis=1) for h in heads], axis=0)
                oc_s[q, seg(g, 128), :] = (gc_s[q, seg(g, 128), :] * mixed).astype(BF16)
        loop(quads, middle, U_CM)

        def after(q):
            update = dot_tn(oc_s[q], w_co[:])
            x = y1[pl.ds(4 * q, 4)].reshape(tokens, width).astype(F32)
            y1[pl.ds(4 * q, 4)] = (x + update).astype(BF16).reshape(4, n_seq, width)
        loop(quads, after, U_CA)

        def factors(q):
            y = layer_norm(y1[pl.ds(4 * q, 4)].reshape(tokens, width))
            all_four = dot_nt(w_ac[:], doubled(y)).astype(BF16).astype(F32)
            half = HD // 2
            for r in range(4):
                i = 4 * q + r
                both = all_four[:, seg(r, 128)] * m_t[pl.ds(i, 1), :]
                a = both[0:HD, :]
                at = pl.ds(pl.multiple_of(i * HD, HD), HD)
                a_t[c, 0, at, :] = jnp.where(low, a, 0.0).astype(BF16)
                a_t[c, 1, at, :] = jnp.where(low, 0.0, a).astype(BF16)
                packed = jnp.where(low[0:half], both[HD:HD + half, :], both[HD + half:2 * HD, :])
                c_t[pl.ds(pl.multiple_of(i * half, half), half), :] = packed.astype(BF16)
        loop(quads, factors, U_CF)
        g_c[c, me] = dot(p5[:], c_t[:]).astype(BF16)
        gather_start(g_c, 1, c)
        for db in range(n // 4):
            part = y1[:, seg(db, 16), :].reshape(16 * rows, width)
            s2[c, seg(db, sup), :] = dot(p3t[:], part).astype(BF16)
        exchange_start(s2, r2, 1, c, False)
    loop(crops, columns)

    def bias_send(buf, e, c, w_b):
        def one(i):
            y = layer_norm(z1[c, i])
            yn[c, i] = y
            tmp_b[pl.ds(pl.multiple_of(i * 8, 8), 4), :] = dot_nt(w_b[:], y)
        loop(rows, one, U_LN)
        buf[c, me] = dot(p6[0:blk, :], tmp_b[:].astype(BF16)).astype(BF16)
        gather_start(buf, e, c)

    def outer(c):
        gather_forward(g_c, 1, c)
        gather_wait(g_c, 1, c)

        def unpack(q):
            for sb in range(n // 4):
                part = g_c[c, 4 * sb:4 * sb + 4, pl.ds(pl.multiple_of(blk * q, 16), blk), :].reshape(sup, 128)
                moved = dot(p4[:], part).astype(BF16)
                for i in range(4):
                    c_f[4 * q + i, seg(sb, blk), :] = moved[seg(i, blk), :]
        loop(HD // 2 // 4, unpack, U_UNP)

        def products(fp):
            for half in range(2):
                u = dot_nt(a_t[c, half], c_f[fp])
                for i in range(rows):
                    at = pl.ds(pl.multiple_of(fp * 2 * HD + half * HD, HD), HD)
                    u_s[i, at, :] = (u[seg(i, HD), :] * rn[c, i:i + 1, :]).astype(BF16)
        loop(HD // 2, products, U_PROD)

        def one(i):
            update = dot(w_fet[:], u_s[i])
            z1[c, i] = (z_ref[c, i].astype(F32) + update.T).astype(BF16)
        loop(rows, one, U_OUT)
        bias_send(g_t1, 2, c, w_tsb)
    loop(crops, outer)

    def triangle(buf, e, c, perm, pieces, piece, select, w_t, w_out):
        gather_forward(buf, e, c)
        gather_wait(buf, e, c)
        unpack_bias(buf, c, 0, perm, 0, pieces, piece)
        col = mask_columns(rm_ref[c], select)
        col3 = jnp.concatenate([col] * (2 * length // 128), axis=1)
        for pair in range(2):
            at = two * pair
            bm_tri[:, at:at + two] = dot_nt(eye[:], b_q[at:at + two, :]) * LOG2E + col3
        loop(rows, lambda i: project(yn[c, i], w_t, i), U_TP)
        attend(rows, lambda u: bm_tri[:])

        def after(i):
            x3[i] = (z1[c, i].astype(F32) + dot_tn(o_s[i], w_out[:])).astype(BF16)
        loop(rows, after, U_TA)

    def start_node(c):
        triangle(g_t1, 2, c, p4, 4, blk, eye, w_ts, w_tso)
        for q in range(quads):
            for b in range(blocks):
                part = x3[4 * q:4 * q + 4, seg(b, 64), :].reshape(256, 128)
                s3[c, q, seg(b, 256), :] = dot(p2[:], part).astype(BF16)
        exchange_start(s3, r3, 2, c, True)
    loop(crops, start_node)

    def transposed(c):
        exchange_wait(r3, 2, c, True)
        for q in range(quads):
            for sb in range(n // 4):
                moved = dot(p3[:], r3[c, q, seg(sb, sup), :]).astype(BF16)
                for i in range(rows):
                    at = 64 * q + 16 * sb
                    z1[c, i, at:at + 16, :] = moved[seg(i, 16), :]

        bias_send(g_t2, 3, c, w_teb)
    loop(crops, transposed)

    def end_node(c):
        triangle(g_t2, 3, c, p4e, 4 * quads, 16, tok, w_te, w_teo)
        for q in range(quads):
            for db in range(n // 4):
                part = x3[:, 64 * q + 16 * db:64 * q + 16 * (db + 1), :].reshape(16 * rows, 128)
                s4[c, q, seg(db, sup), :] = dot(p3t[:], part).astype(BF16)
        exchange_start(s4, r4, 3, c, True)
    loop(crops, end_node)

    def finish(c):
        exchange_wait(r2, 1, c, False)
        for b in range(blocks):
            moved = dot(p2t[:], r2[c, seg(b, 256), :]).astype(BF16)
            for i in range(seqs):
                out_m[c, i, seg(b, 64), :] = moved[seg(i, 64), :]
        exchange_wait(r4, 3, c, True)
        for q in range(quads):
            for b in range(blocks):
                moved = dot(p2t[:], r4[c, q, seg(b, 256), :]).astype(BF16)
                for i in range(4):
                    out_z[c, 4 * q + i, seg(b, 64), :] = moved[seg(i, 64), :]
    loop(crops, finish)

    def drain(c):
        for e, buf in enumerate((g_row, g_c, g_t1, g_t2)):
            gather_end(buf, e, c)
        for e, (buf, planes) in enumerate(((s1, False), (s2, False), (s3, True), (s4, True))):
            exchange_end(buf, e, c, planes)
    loop(crops, drain)


def solution(mesh):
    n = mesh.shape[GROUP_AXIS]
    rows_spec = P(PART_AXIS, GROUP_AXIS, None, None)
    in_specs = (rows_spec, rows_spec, P(PART_AXIS, None, None), P(PART_AXIS, None)) + (P(),) * N_WEIGHTS

    def local_block(msa, pair, msa_mask, res_mask, *weights):
        (w_rb, w_r, w_ro, w_c, w_co, w_ac, w_oo, w_tsb, w_ts, w_tso, w_teb, w_te, w_teo) = weights
        crops, seqs, length, width = msa.shape
        rows, pair_width = pair.shape[1], pair.shape[3]
        n_seq = msa_mask.shape[1]
        heads, tri_heads = w_r.shape[2], w_ts.shape[2]
        quads = rows // 4

        def flat_t(w):
            return jnp.transpose(w, (1, 2, 3, 0)).reshape(-1, w.shape[0])

        operands = [
            msa, pair, msa_mask, res_mask.reshape(crops, 1, length),
            w_rb.T, flat_t(w_r), w_ro.reshape(width, width), flat_t(w_c), w_co.reshape(width, width),
            jnp.transpose(w_ac, (1, 2, 0)).reshape(-1, width), w_oo.reshape(-1, pair_width),
            w_tsb.T, flat_t(w_ts), w_tso.reshape(pair_width, pair_width),
            w_teb.T, flat_t(w_te), w_teo.reshape(pair_width, pair_width),
        ]
        p2 = permutation((4, 64), (1, 0))
        p3 = permutation((4, rows, 4), (1, 0, 2))
        p4 = permutation((4, 4, rows), (1, 0, 2))
        p4e = permutation((4, 4, quads, 4), (1, 2, 0, 3))
        p5 = permutation((rows, HD // 2), (1, 0))
        p6 = permutation((rows, heads), (1, 0))
        tok = permutation((n, quads, 4), (1, 0, 2))
        consts = [p2, p2.T, p3, p3.T, p4, p4e, p5, p6, np.eye(length), tok]
        operands += [jnp.asarray(a, BF16) for a in consts]

        vmem = pl.BlockSpec(memory_space=pltpu.VMEM)
        total = n * 4 * rows
        scratch = [
            pltpu.VMEM((crops, n, heads * rows, length), BF16),
            pltpu.VMEM((crops, n, HD // 2 * rows, 128), BF16),
            pltpu.VMEM((crops, n, tri_heads * rows, length), BF16),
            pltpu.VMEM((crops, n, tri_heads * rows, length), BF16),
        ]
        scratch += [pltpu.VMEM((crops, total, width), BF16)] * 4
        scratch += [pltpu.VMEM((crops, quads, total, pair_width), BF16)] * 4
        scratch += [
            pltpu.VMEM((8 * rows, length), F32),
            pltpu.VMEM((heads * length, length), BF16),
            pltpu.VMEM((width // 128, length, 4 * length), F32),
            pltpu.VMEM((length, tri_heads * length), F32),
            pltpu.VMEM((seqs, length, width), BF16),
            pltpu.VMEM((rows, n_seq, width), BF16),
            pltpu.VMEM((16, 2 * n_seq), F32),
            pltpu.VMEM((crops, 16, length), F32),
            pltpu.VMEM((crops, 2, rows * HD, 128), BF16),
            pltpu.VMEM((rows * HD // 2, 128), BF16),
            pltpu.VMEM((HD // 2, length, 128), BF16),
            pltpu.VMEM((rows, HD * HD, length), BF16),
            pltpu.VMEM((HD * HD, pair_width), F32),
            pltpu.VMEM((HD * HD, pair_width), F32),
            pltpu.VMEM((pair_width, HD * HD), BF16),
            pltpu.VMEM((crops, rows, length, pair_width), BF16),
            pltpu.VMEM((crops, rows, length, pair_width), BF16),
            pltpu.VMEM((rows, length, pair_width), BF16),
            pltpu.VMEM((rows, 128, 4 * length), BF16),
            pltpu.VMEM((rows, length, 128), BF16),
            pltpu.VMEM((rows, 128, length), BF16),
            pltpu.VMEM((rows, 128, length), F32),
            pltpu.VMEM((rows, 128, length), BF16),
            pltpu.VMEM((2, length, 4 * length), F32),
            pltpu.VMEM((seqs, length, 128), F32),
            pltpu.VMEM((quads, width, 8 * n_seq), BF16),
            pltpu.VMEM((quads, 4 * n_seq, width), BF16),
            pltpu.VMEM((quads, 4 * n_seq, width), BF16),
            pltpu.VMEM((quads, width, 4 * n_seq), F32),
            pltpu.VMEM((quads, width, 4 * n_seq), BF16),
            pltpu.VMEM((rows, n_seq, 128), F32),
        ]
        scratch += [pltpu.SemaphoreType.DMA((4, crops))] * 6
        return pl.pallas_call(
            functools.partial(block_kernel, n),
            out_shape=(jax.ShapeDtypeStruct(msa.shape, BF16), jax.ShapeDtypeStruct(pair.shape, BF16)),
            in_specs=[vmem] * len(operands),
            out_specs=(vmem, vmem),
            scratch_shapes=scratch,
            compiler_params=pltpu.CompilerParams(collective_id=0, has_side_effects=True, vmem_limit_bytes=VMEM_BYTES),
            name='evoformer_block',
        )(*operands)

    return jax.shard_map(local_block, mesh=mesh, in_specs=in_specs, out_specs=(rows_spec, rows_spec),
                         check_vma=False)
```

time: 226 us -> 185 us (0.82); the launches traced: 223 us -> 185 us
  Pallas kernels: 218 us -> 180 us
    pallas_call x1, Pallas kernels: 218 us -> 180 us  [local_block(): pl.pallas_call(functools.partial(block_kernel, n), out_shape=(jax.ShapeDt...]
where the time goes in v2:
time: 185 us
  Pallas kernels  180 us (97%)
  local copies, waits for them, and re-layouts  4.44 us (2%)
    pallas_call x1, Pallas kernels, local_block(): pl.pallas_call(functools.partial(block_kernel, n), out_shape=(jax.ShapeDt...  180 us

profile of v2, /device:TPU:21, one launch (start us, length us, event | category | flops | bytes accessed | tf_op | source)
XLA Modules:
  0.0 184.8 jit_solution(6829316472515283928)
XLA Ops:
  0.6 1.3 reshape.37.rm_ref
  1.9 179.7 %evoformer_block.1 = (bf16[2,4,192,256]{3,2,1,0:T(8,128)(2,1)}, bf16[2,12,192,128]{3,2,1,0:T(8,128)(2,1)}) custom-call(bf16[2,4,192,256]{3,2,1,0:T(8,128)(2,1)} %x_ref.1, bf16[2,12,192,128]{3,2,1,0:T(8,128)(2,1)} %z_ref.1, s32[2,64,192]{2,1,0:T(8,128)} %mm_ref.1, s32[2,1,192]{2,1,0:T(1,128)} %reshape.37.rm_ref, bf16[8,128]{1,0:T(8,128)(2,1)} %bitcast.33, ...), custom_call_target="tpu_custom_call" | custom-call | tf_op jit(solution)/shard_map/evoformer_block/pallas_call | solution.py:530
  181.6 0.0 copy-start
  181.6 2.2 %copy.31 = bf16[2,4,192,256]{3,2,1,0:T(8,128)(2,1)} copy(bf16[2,4,192,256]{3,2,1,0:T(8,128)(2,1)} %get-tuple-element.4) | data formatting | bytes 1572864
  183.8 0.0 copy-done
  183.8 1.0 copy.32
Async XLA Ops:
  181.6 2.2 %copy-start = (bf16[2,12,192,128]{3,2,1,0:T(8,128)(2,1)S(1)}, bf16[2,12,192,128]{3,2,1,0:T(8,128)(2,1)}, u32[]{:S(2)}) copy-start(bf16[2,12,192,128]{3,2,1,0:T(8,128)(2,1)} %get-tuple-element.5) | copy-start | bytes 3538948

commit v3 on v2

--- a/solution.py
+++ b/solution.py
@@ -75,12 +75,12 @@
 
 def block_kernel(n, x_ref, z_ref, mm_ref, rm_ref,
                  w_rb, w_r, w_ro, w_c, w_co, w_ac, w_oo, w_tsb, w_ts, w_tso, w_teb, w_te, w_teo,
-                 p2, p2t, p3, p3t, p4, p4e, p5, p6, eye, tok,
+                 p2, p2t, p3, p3t, p4, p4e, p5, p6, p64, eye, tok, tok_l, tok_r,
                  out_m, out_z,
                  g_row, g_c, g_t1, g_t2, s1, r1, s2, r2, s3, r3, s4, r4,
                  tmp_b, b_q, bm_row, bm_tri, x1, y1, m_t, rn, a_t, c_t, c_f, u_s, w_f32, w_fe, w_fet, z1, yn, x3,
                  q_s, k_s, v_s, g_s, o_s, s_buf, m_s, qc_s, kc_s, vc_s, gc_s, oc_s, mc_s,
-                 gs_a, gr_a, gs_b, gr_b, as_sem, ar_sem):
+                 gs_a, gr_a, gs_b, gr_b, gs_f, gr_f, as_sem, ar_sem):
     me = lax.axis_index(GROUP_AXIS)
     chips = n // 2
     chip = me // 2
@@ -98,11 +98,12 @@
         if chips - k != k:
             steps.append(chips - k)
 
+    near = (1, chips - 1, 2, chips - 2)
+    far = tuple(k for k in steps if k not in near)
+
     barrier = pltpu.get_barrier_semaphore()
     for k in range(1, n):
         pl.semaphore_signal(barrier, inc=1, device_id={GROUP_AXIS: lax.rem(me + k, n)}, device_id_type=MESH)
-    pl.semaphore_wait(barrier, n - 1)
-
     def remote(src, dst, send, recv, device):
         return pltpu.make_async_remote_copy(src_ref=src, dst_ref=dst, send_sem=send, recv_sem=recv,
                                             device_id={GROUP_AXIS: device}, device_id_type=MESH)
@@ -110,44 +111,67 @@
     def same_core(k):
         return 2 * lax.rem(chip + k, chips) + core
 
-    def gather_start(buf, e, c):
-        mine = buf.at[c, me]
-        for k in steps:
-            remote(mine, mine, gs_a.at[e, c], gr_a.at[e, c], same_core(k)).start()
-        remote(mine, mine, gs_b.at[e, c], gr_b.at[e, c], partner).start()
-
     def wait_bytes(ref, sem):
         pltpu.make_async_copy(ref, ref, sem).wait()
 
-    def gather_forward(buf, e, c):
-        wait_bytes(buf.at[c, pl.ds(0, chips - 1)], gr_a.at[e, c])
-        for k in steps:
-            block = buf.at[c, same_core(k)]
-            remote(block, block, gs_b.at[e, c], gr_b.at[e, c], partner).start()
+    def to_partner(block, e, c):
+        remote(block, block, gs_b.at[e, c], gr_b.at[e, c], partner).start()
+
+    def gather_start(buf, e, c, hops):
+        mine = buf.at[c, me]
+        for k in hops:
+            remote(mine, mine, gs_a.at[e, c], gr_a.at[e, c], same_core(k)).start()
+        to_partner(mine, e, c)
+
+    def gather_forward(buf, e, c, hops):
+        wait_bytes(buf.at[c, pl.ds(0, len(hops))], gr_a.at[e, c])
+        for k in hops:
+            to_partner(buf.at[c, same_core(k)], e, c)
+
+    def gather_relay(buf, e, c, hops):
+        wait_bytes(buf.at[c, pl.ds(0, len(hops))], gr_a.at[e, c])
+        height = buf.shape[2]
+        cut = height // 2 // 16 * 16
+        for sign, part in ((1, pl.ds(0, cut)), (-1, pl.ds(cut, height - cut))):
+            source = same_core(chips - 2 * sign)
+            block = buf.at[c, source]
+            remote(block, block, gs_f.at[e, c], gr_f.at[e, c], same_core(chips + sign)).start()
+            half = buf.at[c, source, part]
+            remote(half, half, gs_f.at[e, c], gr_f.at[e, c], same_core(chips + 2 * sign)).start()
+        for k in hops:
+            to_partner(buf.at[c, same_core(k)], e, c)
+
+    def relay_forward(buf, e, c):
+        wait_bytes(buf.at[c, pl.ds(0, len(far))], gr_f.at[e, c])
+        for k in far:
+            to_partner(buf.at[c, same_core(k)], e, c)
 
     def gather_wait(buf, e, c):
         wait_bytes(buf.at[c, pl.ds(0, chips)], gr_b.at[e, c])
 
-    def gather_end(buf, e, c):
-        wait_bytes(buf.at[c, pl.ds(0, chips - 1)], gs_a.at[e, c])
+    def gather_end(buf, e, c, hops):
+        wait_bytes(buf.at[c, pl.ds(0, len(hops))], gs_a.at[e, c])
         wait_bytes(buf.at[c, pl.ds(0, chips)], gs_b.at[e, c])
-
-    def block_of(ref, c, d, planes):
-        where = pl.ds(pl.multiple_of(d * blk, 16), blk)
-        return ref.at[c, :, where, :] if planes else ref.at[c, where, :]
-
-    def exchange_start(src, dst, e, c, planes):
-        here = pl.ds(pl.multiple_of(me * blk, 16), blk)
-        if planes:
-            dst[c, :, here, :] = src[c, :, here, :]
-        else:
-            dst[c, here, :] = src[c, here, :]
-        landing = block_of(dst, c, me, planes)
-        for k in steps:
+        if hops is near:
+            wait_bytes(buf.at[c, pl.ds(0, len(far))], gs_f.at[e, c])
+
+    def rows_of(d, offset=0, height=None):
+        return pl.ds(pl.multiple_of(d * blk + offset, 16), height or blk)
+
+    def exchange_own(src, dst, index_of):
+        dst[index_of(me)] = src[index_of(me)]
+
+    def exchange_part(src, dst, e, c, index_of, hops):
+        landing = dst.at[index_of(me)]
+        for k in hops:
             for other in range(2):
                 d = 2 * lax.rem(chip + k, chips) + (core + other) % 2
-                remote(block_of(src, c, d, planes), landing, as_sem.at[e, c], ar_sem.at[e, c], d).start()
-        remote(block_of(src, c, partner, planes), landing, as_sem.at[e, c], ar_sem.at[e, c], partner).start()
+                if k or other:
+                    remote(src.at[index_of(d)], landing, as_sem.at[e, c], ar_sem.at[e, c], d).start()
+
+    def exchange_start(src, dst, e, c, index_of):
+        exchange_own(src, dst, index_of)
+        exchange_part(src, dst, e, c, index_of, steps + [0])
 
     def others(ref, c, planes):
         where = pl.ds(0, (n - 1) * blk)
@@ -172,9 +196,14 @@
         def one(i):
             tmp_b[pl.ds(pl.multiple_of(i * 8, 8), 8), :] = dot_nt(w_rb[:], layer_norm(z_ref[c, i]))
         loop(rows, one, U_LN)
-        g_row[c, me] = dot(p6[:], tmp_b[:].astype(BF16)).astype(BF16)
-        gather_start(g_row, 0, c)
+        t = dot(p6[:], tmp_b[:].astype(BF16))
+        height = t.shape[0]
+        g_row[c, me, 0:height] = t[:, 0:128].astype(BF16)
+        tail = jnp.concatenate([t[seg(g, blk), 128:length] for g in range(2)], axis=1)
+        g_row[c, me, height:height + blk] = tail.astype(BF16)
     loop(crops, row_bias)
+    pl.semaphore_wait(barrier, n - 1)
+    loop(crops, lambda c: gather_start(g_row, 0, c, steps))
 
     w_f32[:] = w_oo[:].astype(F32)
     for fp in range(HD // 2):
@@ -185,13 +214,12 @@
         w_fet[:, seg(b, 128)] = w_fe[seg(b, 128), :].T.astype(BF16)
     q_s[:] = jnp.zeros_like(q_s)
 
-    def unpack_bias(buf, c, group, perm, first, pieces, piece):
+    def unpack_bias(buf, c, perm, pieces, piece):
         for sb in range(n // 4):
-            part = buf[c, 4 * sb:4 * sb + 4, seg(group, blk), :]
-            moved = dot(perm[:], part.reshape(sup, length)).astype(BF16)
+            moved = dot(perm[:], buf[c, seg(sb, 4)].reshape(sup, length)).astype(BF16)
             for i in range(pieces):
-                at = first + i * (length * 4 // pieces) + sb * piece
-                b_q[at:at + piece, :] = moved[i * piece:(i + 1) * piece, :]
+                at = i * (4 * length // pieces) + sb * piece
+                b_q[at:at + piece, :] = moved[seg(i, piece), :]
 
     def mask_columns(row, select):
         wide = jnp.broadcast_to(row.astype(F32), (128, length)).astype(BF16)
@@ -215,7 +243,7 @@
             v_s[u] = values[seg(g, 128), :]
             g_s[u] = gate[seg(g, 128), :]
 
-    def attend(count, bias_of):
+    def attend(first, count, bias_of):
         def mix(u, probs):
             pieces = []
             for p in range(2):
@@ -226,13 +254,13 @@
         def finish(u, mixed):
             o_s[u] = (g_s[u] * mixed).astype(BF16)
 
-        s_buf[0] = dot(k_s[0], q_s[0])
+        s_buf[0] = dot(k_s[first], q_s[first])
 
         def pair(i):
-            u = 2 * i
+            u = first + 2 * i
             s_buf[1] = dot(k_s[u + 1], q_s[u + 1])
             mixed = mix(u, softmax_cols(s_buf[0] * scale + bias_of(u)))
-            after = jnp.minimum(u + 2, count - 1)
+            after = jnp.minimum(u + 2, first + count - 1)
             s_buf[0] = dot(k_s[after], q_s[after])
             probs = softmax_cols(s_buf[1] * scale + bias_of(u + 1))
             finish(u, mixed)
@@ -242,22 +270,38 @@
     groups = width // 128
 
     def row_attention(c):
-        gather_forward(g_row, 0, c)
-        gather_wait(g_row, 0, c)
-        for group in range(groups):
-            unpack_bias(g_row, c, group, p4, group * four, 4, blk)
-        for pair in range(2 * groups):
-            bm_row[pair // 2, :, two * (pair % 2):two * (pair % 2 + 1)] = \
-                dot_nt(eye[:], b_q[seg(pair, two), :]) * LOG2E
-
         def before(s):
             m_s[s] = mask_columns(mm_ref[c, pl.ds(me * seqs + s, 1), :], eye)
             project(layer_norm(x_ref[c, s]), w_r, s * groups)
         loop(seqs, before, U_PR)
 
+        @pl.when(c == 0)
+        def _():
+            gather_forward(g_row, 0, c, steps)
+        gather_wait(g_row, 0, c)
+        for sb in range(n // 4):
+            for part in range(groups + 1):
+                got = g_row[c, seg(sb, 4), seg(part, blk), :].reshape(sup, 128)
+                moved = dot(p4[:], got).astype(BF16)
+                for i in range(4):
+                    piece = moved[seg(i, blk), :]
+                    at = i * length + sb * blk
+                    if part < groups:
+                        b_q[part * four + at:part * four + at + blk, 0:128] = piece
+                    else:
+                        for g in range(groups):
+                            b_q[g * four + at:g * four + at + blk, 128:length] = piece[:, seg(g, 64)]
+        for pair in range(2 * groups):
+            bm_row[pair // 2, :, two * (pair % 2):two * (pair % 2 + 1)] = \
+                dot_nt(eye[:], b_q[seg(pair, two), :]) * LOG2E
+
         def bias_of(u):
             return bm_row[u % groups] + jnp.concatenate([m_s[u // groups]] * (four // 128), axis=1)
-        attend(seqs * groups, bias_of)
+        attend(0, seqs * groups, bias_of)
+
+        @pl.when(c == 0)
+        def _():
+            gather_forward(g_row, 0, 1, steps)
 
         def after(s):
             gated = jnp.concatenate([o_s[s * groups + g] for g in range(groups)], axis=0)
@@ -266,8 +310,11 @@
         for b in range(blocks):
             part = x1[:, seg(b, 64), :].reshape(256, width)
             s1[c, seg(b, 256), :] = dot(p2[:], part).astype(BF16)
-        exchange_start(s1, r1, 0, c, False)
+        exchange_start(s1, r1, 0, c, lambda d: (c, rows_of(d)))
     loop(crops, row_attention)
+
+    def send_back(c, hops):
+        exchange_part(s2, r2, 1, c, lambda d: (c, rows_of(d)), hops)
 
     def columns(c):
         exchange_wait(r1, 0, c, False)
@@ -298,6 +345,11 @@
             vc_s[q] = dot_nt(y, w_c[2 * width:3 * width, :]).astype(BF16)
             gc_s[q] = sigmoid(dot_nt(w_c[3 * width:4 * width, :], y))
         loop(quads, before, U_CP)
+
+        @pl.when(c == 1)
+        def _():
+            gather_relay(g_c, 1, 0, near)
+            send_back(0, near)
 
         def middle(q):
             zeros = jnp.zeros((64, 128), BF16)
@@ -324,6 +376,11 @@
             y1[pl.ds(4 * q, 4)] = (x + update).astype(BF16).reshape(4, n_seq, width)
         loop(quads, after, U_CA)
 
+        @pl.when(c == 1)
+        def _():
+            relay_forward(g_c, 1, 0)
+            send_back(0, far[:2])
+
         def factors(q):
             y = layer_norm(y1[pl.ds(4 * q, 4)].reshape(tokens, width))
             all_four = dot_nt(w_ac[:], doubled(y)).astype(BF16).astype(F32)
@@ -339,24 +396,25 @@
                 c_t[pl.ds(pl.multiple_of(i * half, half), half), :] = packed.astype(BF16)
         loop(quads, factors, U_CF)
         g_c[c, me] = dot(p5[:], c_t[:]).astype(BF16)
-        gather_start(g_c, 1, c)
+        gather_start(g_c, 1, c, near)
         for db in range(n // 4):
             part = y1[:, seg(db, 16), :].reshape(16 * rows, width)
             s2[c, seg(db, sup), :] = dot(p3t[:], part).astype(BF16)
-        exchange_start(s2, r2, 1, c, False)
+        exchange_own(s2, r2, lambda d: (c, rows_of(d)))
+
+        @pl.when(c == 1)
+        def _():
+            send_back(0, far[2:] + (0,))
     loop(crops, columns)
 
-    def bias_send(buf, e, c, w_b):
-        def one(i):
-            y = layer_norm(z1[c, i])
-            yn[c, i] = y
-            tmp_b[pl.ds(pl.multiple_of(i * 8, 8), 4), :] = dot_nt(w_b[:], y)
-        loop(rows, one, U_LN)
+    def bias_row(i, y, w_b):
+        tmp_b[pl.ds(pl.multiple_of(i * 8, 8), 4), :] = dot_nt(w_b[:], y)
+
+    def bias_send(buf, e, c, hops):
         buf[c, me] = dot(p6[0:blk, :], tmp_b[:].astype(BF16)).astype(BF16)
-        gather_start(buf, e, c)
+        gather_start(buf, e, c, hops)
 
     def outer(c):
-        gather_forward(g_c, 1, c)
         gather_wait(g_c, 1, c)
 
         def unpack(q):
@@ -367,6 +425,11 @@
                     c_f[4 * q + i, seg(sb, blk), :] = moved[seg(i, blk), :]
         loop(HD // 2 // 4, unpack, U_UNP)
 
+        @pl.when(c == 1)
+        def _():
+            gather_relay(g_t1, 2, 0, near)
+            send_back(1, far[:2])
+
         def products(fp):
             for half in range(2):
                 u = dot_nt(a_t[c, half], c_f[fp])
@@ -375,39 +438,77 @@
                     u_s[i, at, :] = (u[seg(i, HD), :] * rn[c, i:i + 1, :]).astype(BF16)
         loop(HD // 2, products, U_PROD)
 
+        @pl.when(c == 1)
+        def _():
+            relay_forward(g_t1, 2, 0)
+            send_back(1, far[2:] + (0,))
+
         def one(i):
             update = dot(w_fet[:], u_s[i])
             z1[c, i] = (z_ref[c, i].astype(F32) + update.T).astype(BF16)
         loop(rows, one, U_OUT)
-        bias_send(g_t1, 2, c, w_tsb)
+
+        @pl.when(c == 0)
+        def _():
+            gather_relay(g_c, 1, 1, near)
+
+        def norm(i):
+            y = layer_norm(z1[c, i])
+            yn[c, i] = y
+            bias_row(i, y, w_tsb)
+        loop(rows, norm, U_LN)
+        bias_send(g_t1, 2, c, near)
+
+        @pl.when(c == 0)
+        def _():
+            send_back(1, near)
+            relay_forward(g_c, 1, 1)
     loop(crops, outer)
 
-    def triangle(buf, e, c, perm, pieces, piece, select, w_t, w_out):
-        gather_forward(buf, e, c)
-        gather_wait(buf, e, c)
-        unpack_bias(buf, c, 0, perm, 0, pieces, piece)
-        col = mask_columns(rm_ref[c], select)
-        col3 = jnp.concatenate([col] * (2 * length // 128), axis=1)
+    def triangle(c, w_out, done):
+        def quad(q):
+            attend(4 * q, 4, lambda u: bm_tri[:])
+
+            def after(k):
+                i = 4 * q + k
+                x3[i] = (z1[c, i].astype(F32) + dot_tn(o_s[i], w_out[:])).astype(BF16)
+            loop(4, after, 4)
+            done(q)
+        loop(quads, quad)
+
+    def start_node(c):
+        loop(rows, lambda i: project(yn[c, i], w_ts, i), U_TP)
+
+        @pl.when(c == 0)
+        def _():
+            gather_relay(g_t1, 2, 1, near)
+        gather_wait(g_t1, 2, c)
+        unpack_bias(g_t1, c, p4, 4, blk)
+        col = mask_columns(rm_ref[pl.ds(c, 1), :], eye)
+        col3 = jnp.concatenate([col] * (two // 128), axis=1)
         for pair in range(2):
-            at = two * pair
-            bm_tri[:, at:at + two] = dot_nt(eye[:], b_q[at:at + two, :]) * LOG2E + col3
-        loop(rows, lambda i: project(yn[c, i], w_t, i), U_TP)
-        attend(rows, lambda u: bm_tri[:])
-
-        def after(i):
-            x3[i] = (z1[c, i].astype(F32) + dot_tn(o_s[i], w_out[:])).astype(BF16)
-        loop(rows, after, U_TA)
-
-    def start_node(c):
-        triangle(g_t1, 2, c, p4, 4, blk, eye, w_ts, w_tso)
-        for q in range(quads):
+            bm_tri[:, seg(pair, two)] = dot_nt(eye[:], b_q[seg(pair, two), :]) * LOG2E + col3
+
+        def done(q):
+            for k in range(4):
+                i = 4 * q + k
+                bias_row(i, layer_norm(x3[i]), w_teb)
+
+            @pl.when(q == quads - 1)
+            def _():
+                bias_send(g_t2, 3, c, steps)
             for b in range(blocks):
-                part = x3[4 * q:4 * q + 4, seg(b, 64), :].reshape(256, 128)
+                part = x3[pl.ds(4 * q, 4), seg(b, 64), :].reshape(256, 128)
                 s3[c, q, seg(b, 256), :] = dot(p2[:], part).astype(BF16)
-        exchange_start(s3, r3, 2, c, True)
+            exchange_start(s3, r3, 2, c, lambda d: (c, q, rows_of(d)))
+
+            @pl.when((c == 0) & (q == 0))
+            def _():
+                relay_forward(g_t1, 2, 1)
+        triangle(c, w_tso, done)
     loop(crops, start_node)
 
-    def transposed(c):
+    def end_node(c):
         exchange_wait(r3, 2, c, True)
         for q in range(quads):
             for sb in range(n // 4):
@@ -415,36 +516,48 @@
                 for i in range(rows):
                     at = 64 * q + 16 * sb
                     z1[c, i, at:at + 16, :] = moved[seg(i, 16), :]
-
-        bias_send(g_t2, 3, c, w_teb)
-    loop(crops, transposed)
-
-    def end_node(c):
-        triangle(g_t2, 3, c, p4e, 4 * quads, 16, tok, w_te, w_teo)
-        for q in range(quads):
-            for db in range(n // 4):
-                part = x3[:, 64 * q + 16 * db:64 * q + 16 * (db + 1), :].reshape(16 * rows, 128)
-                s4[c, q, seg(db, sup), :] = dot(p3t[:], part).astype(BF16)
-        exchange_start(s4, r4, 3, c, True)
+        loop(rows, lambda i: project(layer_norm(z1[c, i]), w_te, i), U_TP)
+        gather_forward(g_t2, 3, c, steps)
+        gather_wait(g_t2, 3, c)
+        unpack_bias(g_t2, c, p4e, 4 * quads, 16)
+        col = mask_columns(rm_ref[pl.ds(c, 1), :], tok)
+        col3 = jnp.concatenate([col] * (two // 128), axis=1)
+        for pair in range(2):
+            left = dot_nt(b_q[seg(2 * pair, length), :], tok_l[:])
+            right = dot_nt(b_q[seg(2 * pair + 1, length), :], tok_r[:])
+            bm_tri[:, seg(pair, two)] = (left + right) * LOG2E + col3
+
+        def done(q):
+            for p in range(quads):
+                for db in range(n // 4):
+                    part = x3[pl.ds(4 * q, 4), 64 * p + 16 * db:64 * p + 16 * (db + 1), :].reshape(64, 128)
+                    moved = dot(p64[:], part).astype(BF16)
+                    for i in range(4):
+                        s4[c, p, rows_of(4 * db + i, 16 * q, 16), :] = moved[seg(i, 16), :]
+            exchange_start(s4, r4, 3, c, lambda d: (c, slice(None), rows_of(d, 16 * q, 16)))
+        triangle(c, w_teo, done)
     loop(crops, end_node)
 
-    def finish(c):
+    def finish_msa(c):
         exchange_wait(r2, 1, c, False)
         for b in range(blocks):
             moved = dot(p2t[:], r2[c, seg(b, 256), :]).astype(BF16)
             for i in range(seqs):
                 out_m[c, i, seg(b, 64), :] = moved[seg(i, 64), :]
+    loop(crops, finish_msa)
+
+    def finish_pair(c):
         exchange_wait(r4, 3, c, True)
         for q in range(quads):
             for b in range(blocks):
                 moved = dot(p2t[:], r4[c, q, seg(b, 256), :]).astype(BF16)
                 for i in range(4):
                     out_z[c, 4 * q + i, seg(b, 64), :] = moved[seg(i, 64), :]
-    loop(crops, finish)
+    loop(crops, finish_pair)
 
     def drain(c):
-        for e, buf in enumerate((g_row, g_c, g_t1, g_t2)):
-            gather_end(buf, e, c)
+        for e, (buf, hops) in enumerate(((g_row, steps), (g_c, near), (g_t1, near), (g_t2, steps))):
+            gather_end(buf, e, c, hops)
         for e, (buf, planes) in enumerate(((s1, False), (s2, False), (s3, True), (s4, True))):
             exchange_end(buf, e, c, planes)
     loop(crops, drain)
@@ -467,7 +580,7 @@
             return jnp.transpose(w, (1, 2, 3, 0)).reshape(-1, w.shape[0])
 
         operands = [
-            msa, pair, msa_mask, res_mask.reshape(crops, 1, length),
+            msa, pair, msa_mask, res_mask,
             w_rb.T, flat_t(w_r), w_ro.reshape(width, width), flat_t(w_c), w_co.reshape(width, width),
             jnp.transpose(w_ac, (1, 2, 0)).reshape(-1, width), w_oo.reshape(-1, pair_width),
             w_tsb.T, flat_t(w_ts), w_tso.reshape(pair_width, pair_width),
@@ -479,14 +592,16 @@
         p4e = permutation((4, 4, quads, 4), (1, 2, 0, 3))
         p5 = permutation((rows, HD // 2), (1, 0))
         p6 = permutation((rows, heads), (1, 0))
+        p64 = permutation((4, 4, 4), (1, 0, 2))
         tok = permutation((n, quads, 4), (1, 0, 2))
-        consts = [p2, p2.T, p3, p3.T, p4, p4e, p5, p6, np.eye(length), tok]
+        consts = [p2, p2.T, p3, p3.T, p4, p4e, p5, p6, p64, np.eye(length), tok,
+                  np.concatenate([tok, 0 * tok]), np.concatenate([0 * tok, tok])]
         operands += [jnp.asarray(a, BF16) for a in consts]
 
         vmem = pl.BlockSpec(memory_space=pltpu.VMEM)
         total = n * 4 * rows
         scratch = [
-            pltpu.VMEM((crops, n, heads * rows, length), BF16),
+            pltpu.VMEM((crops, n, heads * rows + 4 * rows, 128), BF16),
             pltpu.VMEM((crops, n, HD // 2 * rows, 128), BF16),
             pltpu.VMEM((crops, n, tri_heads * rows, length), BF16),
             pltpu.VMEM((crops, n, tri_heads * rows, length), BF16),
@@ -526,7 +641,7 @@
             pltpu.VMEM((quads, width, 4 * n_seq), BF16),
             pltpu.VMEM((rows, n_seq, 128), F32),
         ]
-        scratch += [pltpu.SemaphoreType.DMA((4, crops))] * 6
+        scratch += [pltpu.SemaphoreType.DMA((4, crops))] * 8
         return pl.pallas_call(
             functools.partial(block_kernel, n),
             out_shape=(jax.ShapeDtypeStruct(msa.shape, BF16), jax.ShapeDtypeStruct(pair.shape, BF16)),

time: 185 us -> 166 us (0.90)
  Pallas kernels: 180 us -> 161 us
    pallas_call x1, Pallas kernels: 180 us -> 161 us  [local_block(): pl.pallas_call(functools.partial(block_kernel, n), out_shape=(jax.ShapeDt...]
where the time goes in v3:
time: 166 us; the launch traced here: 165 us
  Pallas kernels  161 us (97%)
  local copies, waits for them, and re-layouts  3.18 us (2%)
    pallas_call x1, Pallas kernels, local_block(): pl.pallas_call(functools.partial(block_kernel, n), out_shape=(jax.ShapeDt...  161 us

profile of v3, /device:TPU:21, one launch (start us, length us, event | category | flops | bytes accessed | tf_op | source)
XLA Modules:
  0.0 164.9 jit_solution(11795680702912792806)
XLA Ops:
  0.6 161.0 %evoformer_block.1 = (bf16[2,4,192,256]{3,2,1,0:T(8,128)(2,1)}, bf16[2,12,192,128]{3,2,1,0:T(8,128)(2,1)}) custom-call(bf16[2,4,192,256]{3,2,1,0:T(8,128)(2,1)} %x_ref.1, bf16[2,12,192,128]{3,2,1,0:T(8,128)(2,1)} %z_ref.1, s32[2,64,192]{2,1,0:T(8,128)} %mm_ref.1, s32[2,192]{1,0:T(2,128)} %rm_ref.1, bf16[8,128]{1,0:T(8,128)(2,1)} %bitcast.33, ...), custom_call_target="tpu_custom_call" | custom-call | tf_op jit(solution)/shard_map/evoformer_block/pallas_call | solution.py:645
  161.7 0.0 copy-start
  161.7 2.2 %copy.34 = bf16[2,4,192,256]{3,2,1,0:T(8,128)(2,1)} copy(bf16[2,4,192,256]{3,2,1,0:T(8,128)(2,1)} %get-tuple-element.4) | data formatting | bytes 1572864
  163.8 0.0 copy-done
  163.8 1.0 copy.35
Async XLA Ops:
  161.7 2.2 %copy-start = (bf16[2,12,192,128]{3,2,1,0:T(8,128)(2,1)S(1)}, bf16[2,12,192,128]{3,2,1,0:T(8,128)(2,1)}, u32[]{:S(2)}) copy-start(bf16[2,12,192,128]{3,2,1,0:T(8,128)(2,1)} %get-tuple-element.5) | copy-start | bytes 3538948

commit v4 on v3

--- a/solution.py
+++ b/solution.py
@@ -75,13 +75,14 @@
 
 def block_kernel(n, x_ref, z_ref, mm_ref, rm_ref,
                  w_rb, w_r, w_ro, w_c, w_co, w_ac, w_oo, w_tsb, w_ts, w_tso, w_teb, w_te, w_teo,
-                 p2, p2t, p3, p3t, p4, p4e, p5, p6, p64, eye, tok, tok_l, tok_r,
+                 p2, p2t, p3, p3t, p4, p4b, p4e, p4eb, p5, p6, p64, eye, tok, tok_l, tok_r,
                  out_m, out_z,
-                 g_row, g_c, g_t1, g_t2, s1, r1, s2, r2, s3, r3, s4, r4,
-                 tmp_b, b_q, bm_row, bm_tri, x1, y1, m_t, rn, a_t, c_t, c_f, u_s, w_f32, w_fe, w_fet, z1, yn, x3,
+                 g_r0, g_r1, g_c, g_t1, g_t2, s1, r1, s2, r2, s3, r3, s4, r4,
+                 tmp_b, b_q, bm_tri, x1, y1, m_t, rn, a_t, c_t, c_f, u_s, w_f32, w_fe, w_fet, z1, yn, x3,
                  q_s, k_s, v_s, g_s, o_s, s_buf, m_s, qc_s, kc_s, vc_s, gc_s, oc_s, mc_s,
                  gs_a, gr_a, gs_b, gr_b, gs_f, gr_f, as_sem, ar_sem):
     me = lax.axis_index(GROUP_AXIS)
+    g_row = (g_r0, g_r1)
     chips = n // 2
     chip = me // 2
     core = me % 2
@@ -190,6 +191,11 @@
             return carry
         lax.fori_loop(0, count // unroll, several, 0)
 
+    def pack_bias(rows_f32):
+        half = blk // 2
+        last = jnp.concatenate([rows_f32[seg(g, half), 128:length] for g in range(2)], axis=1)
+        return jnp.concatenate([rows_f32[:, 0:128], last, jnp.zeros((8, 128), F32)], axis=0).astype(BF16)
+
     tmp_b[:] = jnp.zeros_like(tmp_b)
 
     def row_bias(c):
@@ -197,13 +203,15 @@
             tmp_b[pl.ds(pl.multiple_of(i * 8, 8), 8), :] = dot_nt(w_rb[:], layer_norm(z_ref[c, i]))
         loop(rows, one, U_LN)
         t = dot(p6[:], tmp_b[:].astype(BF16))
-        height = t.shape[0]
-        g_row[c, me, 0:height] = t[:, 0:128].astype(BF16)
-        tail = jnp.concatenate([t[seg(g, blk), 128:length] for g in range(2)], axis=1)
-        g_row[c, me, height:height + blk] = tail.astype(BF16)
+        for g, buf in enumerate(g_row):
+            buf[c, me] = pack_bias(t[seg(g, blk), :])
     loop(crops, row_bias)
     pl.semaphore_wait(barrier, n - 1)
-    loop(crops, lambda c: gather_start(g_row, 0, c, steps))
+
+    def row_bias_send(c):
+        for g, buf in enumerate(g_row):
+            gather_start(buf, g, c, steps)
+    loop(crops, row_bias_send)
 
     w_f32[:] = w_oo[:].astype(F32)
     for fp in range(HD // 2):
@@ -214,12 +222,14 @@
         w_fet[:, seg(b, 128)] = w_fe[seg(b, 128), :].T.astype(BF16)
     q_s[:] = jnp.zeros_like(q_s)
 
-    def unpack_bias(buf, c, perm, pieces, piece):
+    def unpack_bias(buf, c, perm, perm_last, pieces, piece):
         for sb in range(n // 4):
-            moved = dot(perm[:], buf[c, seg(sb, 4)].reshape(sup, length)).astype(BF16)
+            moved = dot(perm[:], buf[c, seg(sb, 4), 0:blk, :].reshape(sup, 128)).astype(BF16)
+            last = dot(perm_last[:], buf[c, seg(sb, 4), blk:, :].reshape(128, 128)).astype(BF16)
             for i in range(pieces):
                 at = i * (4 * length // pieces) + sb * piece
-                b_q[at:at + piece, :] = moved[seg(i, piece), :]
+                b_q[at:at + piece, 0:128] = moved[seg(i, piece), :]
+                b_q[at:at + piece, 128:length] = last[seg(i % (pieces // 2), piece), seg(2 * i // pieces, 64)]
 
     def mask_columns(row, select):
         wide = jnp.broadcast_to(row.astype(F32), (128, length)).astype(BF16)
@@ -228,7 +238,7 @@
     scale = HD ** -0.5 * LOG2E
     two, four = 2 * length, 4 * length
 
-    def project(y, w_t, first):
+    def project(y, w_t, first, stride=1):
         wide = y.shape[1]
         q = dot_nt(w_t[0:wide, :], jnp.concatenate([y, y], axis=0))
         q = jnp.where(same_half(wide, two, length), q, 0.0).astype(BF16)
@@ -236,7 +246,7 @@
         values = dot_nt(w_t[2 * wide:3 * wide, :], y).astype(BF16)
         gate = sigmoid(dot_nt(w_t[3 * wide:4 * wide, :], y))
         for g in range(wide // 128):
-            u = first + g
+            u = first + g * stride
             q_s[u, 0:64, 0:two] = q[128 * g:128 * g + 64, :]
             q_s[u, 64:128, two:four] = q[128 * g + 64:128 * g + 128, :]
             k_s[u] = keys[:, seg(g, 128)]
@@ -272,39 +282,21 @@
     def row_attention(c):
         def before(s):
             m_s[s] = mask_columns(mm_ref[c, pl.ds(me * seqs + s, 1), :], eye)
-            project(layer_norm(x_ref[c, s]), w_r, s * groups)
+            project(layer_norm(x_ref[c, s]), w_r, s, seqs)
         loop(seqs, before, U_PR)
-
-        @pl.when(c == 0)
-        def _():
-            gather_forward(g_row, 0, c, steps)
-        gather_wait(g_row, 0, c)
-        for sb in range(n // 4):
-            for part in range(groups + 1):
-                got = g_row[c, seg(sb, 4), seg(part, blk), :].reshape(sup, 128)
-                moved = dot(p4[:], got).astype(BF16)
-                for i in range(4):
-                    piece = moved[seg(i, blk), :]
-                    at = i * length + sb * blk
-                    if part < groups:
-                        b_q[part * four + at:part * four + at + blk, 0:128] = piece
-                    else:
-                        for g in range(groups):
-                            b_q[g * four + at:g * four + at + blk, 128:length] = piece[:, seg(g, 64)]
-        for pair in range(2 * groups):
-            bm_row[pair // 2, :, two * (pair % 2):two * (pair % 2 + 1)] = \
-                dot_nt(eye[:], b_q[seg(pair, two), :]) * LOG2E
-
-        def bias_of(u):
-            return bm_row[u % groups] + jnp.concatenate([m_s[u // groups]] * (four // 128), axis=1)
-        attend(0, seqs * groups, bias_of)
-
-        @pl.when(c == 0)
-        def _():
-            gather_forward(g_row, 0, 1, steps)
+        for g, buf in enumerate(g_row):
+            gather_forward(buf, g, c, steps)
+            gather_wait(buf, g, c)
+            unpack_bias(buf, c, p4, p4b, 4, blk)
+            for pair in range(2):
+                bm_tri[:, seg(pair, two)] = dot_nt(eye[:], b_q[seg(pair, two), :]) * LOG2E
+
+            def bias_of(u):
+                return bm_tri[:] + jnp.concatenate([m_s[u - g * seqs]] * (four // 128), axis=1)
+            attend(g * seqs, seqs, bias_of)
 
         def after(s):
-            gated = jnp.concatenate([o_s[s * groups + g] for g in range(groups)], axis=0)
+            gated = jnp.concatenate([o_s[g * seqs + s] for g in range(groups)], axis=0)
             x1[s] = (x_ref[c, s].astype(F32) + dot_tn(gated, w_ro[:])).astype(BF16)
         loop(seqs, after, U_PO)
         for b in range(blocks):
@@ -348,8 +340,8 @@
 
         @pl.when(c == 1)
         def _():
-            gather_relay(g_c, 1, 0, near)
-            send_back(0, near)
+            gather_relay(g_c, 2, 0, near)
+            send_back(0, near + far[:2])
 
         def middle(q):
             zeros = jnp.zeros((64, 128), BF16)
@@ -378,8 +370,7 @@
 
         @pl.when(c == 1)
         def _():
-            relay_forward(g_c, 1, 0)
-            send_back(0, far[:2])
+            relay_forward(g_c, 2, 0)
 
         def factors(q):
             y = layer_norm(y1[pl.ds(4 * q, 4)].reshape(tokens, width))
@@ -396,26 +387,25 @@
                 c_t[pl.ds(pl.multiple_of(i * half, half), half), :] = packed.astype(BF16)
         loop(quads, factors, U_CF)
         g_c[c, me] = dot(p5[:], c_t[:]).astype(BF16)
-        gather_start(g_c, 1, c, near)
+        gather_start(g_c, 2, c, near)
         for db in range(n // 4):
             part = y1[:, seg(db, 16), :].reshape(16 * rows, width)
             s2[c, seg(db, sup), :] = dot(p3t[:], part).astype(BF16)
         exchange_own(s2, r2, lambda d: (c, rows_of(d)))
-
-        @pl.when(c == 1)
-        def _():
-            send_back(0, far[2:] + (0,))
     loop(crops, columns)
 
     def bias_row(i, y, w_b):
         tmp_b[pl.ds(pl.multiple_of(i * 8, 8), 4), :] = dot_nt(w_b[:], y)
 
     def bias_send(buf, e, c, hops):
-        buf[c, me] = dot(p6[0:blk, :], tmp_b[:].astype(BF16)).astype(BF16)
+        buf[c, me] = pack_bias(dot(p6[0:blk, :], tmp_b[:].astype(BF16)))
         gather_start(buf, e, c, hops)
 
+    def start_project(c):
+        loop(rows, lambda i: project(yn[c, i], w_ts, i), U_TP)
+
     def outer(c):
-        gather_wait(g_c, 1, c)
+        gather_wait(g_c, 2, c)
 
         def unpack(q):
             for sb in range(n // 4):
@@ -425,11 +415,6 @@
                     c_f[4 * q + i, seg(sb, blk), :] = moved[seg(i, blk), :]
         loop(HD // 2 // 4, unpack, U_UNP)
 
-        @pl.when(c == 1)
-        def _():
-            gather_relay(g_t1, 2, 0, near)
-            send_back(1, far[:2])
-
         def products(fp):
             for half in range(2):
                 u = dot_nt(a_t[c, half], c_f[fp])
@@ -440,8 +425,7 @@
 
         @pl.when(c == 1)
         def _():
-            relay_forward(g_t1, 2, 0)
-            send_back(1, far[2:] + (0,))
+            send_back(1, near + far[:2])
 
         def one(i):
             update = dot(w_fet[:], u_s[i])
@@ -450,19 +434,24 @@
 
         @pl.when(c == 0)
         def _():
-            gather_relay(g_c, 1, 1, near)
+            gather_relay(g_c, 2, 1, near)
 
         def norm(i):
             y = layer_norm(z1[c, i])
             yn[c, i] = y
             bias_row(i, y, w_tsb)
         loop(rows, norm, U_LN)
-        bias_send(g_t1, 2, c, near)
 
         @pl.when(c == 0)
         def _():
-            send_back(1, near)
-            relay_forward(g_c, 1, 1)
+            start_project(0)
+            relay_forward(g_c, 2, 1)
+        bias_send(g_t1, 3, c, steps)
+        send_back(c, far[2:] + (0,))
+
+        @pl.when(c == 1)
+        def _():
+            gather_forward(g_t1, 3, 0, steps)
     loop(crops, outer)
 
     def triangle(c, w_out, done):
@@ -477,13 +466,12 @@
         loop(quads, quad)
 
     def start_node(c):
-        loop(rows, lambda i: project(yn[c, i], w_ts, i), U_TP)
-
-        @pl.when(c == 0)
+        @pl.when(c == 1)
         def _():
-            gather_relay(g_t1, 2, 1, near)
-        gather_wait(g_t1, 2, c)
-        unpack_bias(g_t1, c, p4, 4, blk)
+            start_project(1)
+            gather_forward(g_t1, 3, 1, steps)
+        gather_wait(g_t1, 3, c)
+        unpack_bias(g_t1, c, p4, p4b, 4, blk)
         col = mask_columns(rm_ref[pl.ds(c, 1), :], eye)
         col3 = jnp.concatenate([col] * (two // 128), axis=1)
         for pair in range(2):
@@ -496,15 +484,11 @@
 
             @pl.when(q == quads - 1)
             def _():
-                bias_send(g_t2, 3, c, steps)
+                bias_send(g_t2, 4, c, steps)
             for b in range(blocks):
                 part = x3[pl.ds(4 * q, 4), seg(b, 64), :].reshape(256, 128)
                 s3[c, q, seg(b, 256), :] = dot(p2[:], part).astype(BF16)
             exchange_start(s3, r3, 2, c, lambda d: (c, q, rows_of(d)))
-
-            @pl.when((c == 0) & (q == 0))
-            def _():
-                relay_forward(g_t1, 2, 1)
         triangle(c, w_tso, done)
     loop(crops, start_node)
 
@@ -517,9 +501,9 @@
                     at = 64 * q + 16 * sb
                     z1[c, i, at:at + 16, :] = moved[seg(i, 16), :]
         loop(rows, lambda i: project(layer_norm(z1[c, i]), w_te, i), U_TP)
-        gather_forward(g_t2, 3, c, steps)
-        gather_wait(g_t2, 3, c)
-        unpack_bias(g_t2, c, p4e, 4 * quads, 16)
+        gather_forward(g_t2, 4, c, steps)
+        gather_wait(g_t2, 4, c)
+        unpack_bias(g_t2, c, p4e, p4eb, 4 * quads, 16)
         col = mask_columns(rm_ref[pl.ds(c, 1), :], tok)
         col3 = jnp.concatenate([col] * (two // 128), axis=1)
         for pair in range(2):
@@ -556,7 +540,7 @@
     loop(crops, finish_pair)
 
     def drain(c):
-        for e, (buf, hops) in enumerate(((g_row, steps), (g_c, near), (g_t1, near), (g_t2, steps))):
+        for e, (buf, hops) in enumerate([(b, steps) for b in g_row] + [(g_c, near), (g_t1, steps), (g_t2, steps)]):
             gather_end(buf, e, c, hops)
         for e, (buf, planes) in enumerate(((s1, False), (s2, False), (s3, True), (s4, True))):
             exchange_end(buf, e, c, planes)
@@ -590,28 +574,31 @@
         p3 = permutation((4, rows, 4), (1, 0, 2))
         p4 = permutation((4, 4, rows), (1, 0, 2))
         p4e = permutation((4, 4, quads, 4), (1, 2, 0, 3))
+
+        def last(p):
+            half = p[:len(p) // 2].reshape(-1, 4, 4 * rows)[:, :, :2 * rows]
+            return np.pad(half, ((0, 0), (0, 0), (0, 32 - 2 * rows))).reshape(len(p) // 2, -1)
         p5 = permutation((rows, HD // 2), (1, 0))
         p6 = permutation((rows, heads), (1, 0))
         p64 = permutation((4, 4, 4), (1, 0, 2))
         tok = permutation((n, quads, 4), (1, 0, 2))
-        consts = [p2, p2.T, p3, p3.T, p4, p4e, p5, p6, p64, np.eye(length), tok,
+        consts = [p2, p2.T, p3, p3.T, p4, last(p4), p4e, last(p4e), p5, p6, p64, np.eye(length), tok,
                   np.concatenate([tok, 0 * tok]), np.concatenate([0 * tok, tok])]
         operands += [jnp.asarray(a, BF16) for a in consts]
 
         vmem = pl.BlockSpec(memory_space=pltpu.VMEM)
         total = n * 4 * rows
+        bias = pltpu.VMEM((crops, n, 4 * rows + 32, 128), BF16)
         scratch = [
-            pltpu.VMEM((crops, n, heads * rows + 4 * rows, 128), BF16),
+            bias, bias,
             pltpu.VMEM((crops, n, HD // 2 * rows, 128), BF16),
-            pltpu.VMEM((crops, n, tri_heads * rows, length), BF16),
-            pltpu.VMEM((crops, n, tri_heads * rows, length), BF16),
+            bias, bias,
         ]
         scratch += [pltpu.VMEM((crops, total, width), BF16)] * 4
         scratch += [pltpu.VMEM((crops, quads, total, pair_width), BF16)] * 4
         scratch += [
             pltpu.VMEM((8 * rows, length), F32),
-            pltpu.VMEM((heads * length, length), BF16),
-            pltpu.VMEM((width // 128, length, 4 * length), F32),
+            pltpu.VMEM((tri_heads * length, length), BF16),
             pltpu.VMEM((length, tri_heads * length), F32),
             pltpu.VMEM((seqs, length, width), BF16),
             pltpu.VMEM((rows, n_seq, width), BF16),
@@ -641,7 +628,7 @@
             pltpu.VMEM((quads, width, 4 * n_seq), BF16),
             pltpu.VMEM((rows, n_seq, 128), F32),
         ]
-        scratch += [pltpu.SemaphoreType.DMA((4, crops))] * 8
+        scratch += [pltpu.SemaphoreType.DMA((5, crops))] * 8
         return pl.pallas_call(
             functools.partial(block_kernel, n),
             out_shape=(jax.ShapeDtypeStruct(msa.shape, BF16), jax.ShapeDtypeStruct(pair.shape, BF16)),

time: 166 us -> 158 us (0.952)
  Pallas kernels: 161 us -> 153 us
    pallas_call x1, Pallas kernels: 161 us -> 153 us  [local_block(): pl.pallas_call(functools.partial(block_kernel, n), out_shape=(jax.ShapeDt...]
where the time goes in v4:
time: 158 us; the launch traced here: 157 us
  Pallas kernels  153 us (97%)
  local copies, waits for them, and re-layouts  3.18 us (2%)
    pallas_call x1, Pallas kernels, local_block(): pl.pallas_call(functools.partial(block_kernel, n), out_shape=(jax.ShapeDt...  153 us
    unnamed x4, local copies, waits for them, and re-layouts  3.18 us

profile of v4, /device:TPU:21, one launch (start us, length us, event | category | flops | bytes accessed | tf_op | source)
XLA Modules:
  0.0 156.8 jit_solution(13948219136726437199)
XLA Ops:
  0.6 152.9 %evoformer_block.1 = (bf16[2,4,192,256]{3,2,1,0:T(8,128)(2,1)}, bf16[2,12,192,128]{3,2,1,0:T(8,128)(2,1)}) custom-call(bf16[2,4,192,256]{3,2,1,0:T(8,128)(2,1)} %x_ref.1, bf16[2,12,192,128]{3,2,1,0:T(8,128)(2,1)} %z_ref.1, s32[2,64,192]{2,1,0:T(8,128)} %mm_ref.1, s32[2,192]{1,0:T(2,128)} %rm_ref.1, bf16[8,128]{1,0:T(8,128)(2,1)} %bitcast.33, ...), custom_call_target="tpu_custom_call" | custom-call | tf_op jit(solution)/shard_map/evoformer_block/pallas_call | solution.py:632
  153.6 0.0 copy-start
  153.6 2.2 %copy.36 = bf16[2,4,192,256]{3,2,1,0:T(8,128)(2,1)} copy(bf16[2,4,192,256]{3,2,1,0:T(8,128)(2,1)} %get-tuple-element.4) | data formatting | bytes 1572864
  155.7 0.0 copy-done
  155.7 1.0 copy.37
Async XLA Ops:
  153.6 2.2 %copy-start = (bf16[2,12,192,128]{3,2,1,0:T(8,128)(2,1)S(1)}, bf16[2,12,192,128]{3,2,1,0:T(8,128)(2,1)}, u32[]{:S(2)}) copy-start(bf16[2,12,192,128]{3,2,1,0:T(8,128)(2,1)} %get-tuple-element.5) | copy-start | bytes 3538948

commit v5 on v4

--- a/solution.py
+++ b/solution.py
@@ -21,7 +21,7 @@
 BF16 = jnp.bfloat16
 HD = 32
 U_LN, U_UNP, U_PROD, U_OUT = 12, 2, 4, 3
-U_PR, U_PO, U_TP, U_TA, U_CP, U_CM, U_CA, U_CF = 2, 4, 3, 4, 1, 1, 3, 3
+U_PR, U_PO, U_TP, U_CP, U_CM, U_CF = 2, 4, 3, 3, 3, 3
 VMEM_BYTES = 60 * 1024 * 1024
 
 
@@ -94,13 +94,11 @@
     blk = 4 * rows
     sup = 4 * blk
     steps = []
-    for k in range(1, chips // 2 + 1):
-        steps.append(k)
-        if chips - k != k:
-            steps.append(chips - k)
-
-    near = (1, chips - 1, 2, chips - 2)
+    for k in range(chips // 2, 0, -1):
+        steps += [k] if chips - k == k else [chips - k, k]
+    near = (2, chips - 2, 1, chips - 1)
     far = tuple(k for k in steps if k not in near)
+    middle_hops, last_hops = far[1:], far[:1] + (0,)
 
     barrier = pltpu.get_barrier_semaphore()
     for k in range(1, n):
@@ -275,7 +273,7 @@
             probs = softmax_cols(s_buf[1] * scale + bias_of(u + 1))
             finish(u, mixed)
             finish(u + 1, mix(u + 1, probs))
-        loop(count // 2, pair)
+        loop(count // 2, pair, 2)
 
     groups = width // 128
 
@@ -320,10 +318,9 @@
         m_t[:] = dot_nt(mine, jnp.concatenate([mk, mk], axis=0))
         rn[c] = 1.0 / (dot(m_t[:, 0:n_seq].astype(BF16), mk) + OPM_EPS)
         low = iota((HD, 2 * n_seq), 1) < n_seq
-        picks = (iota((128 * rows, length), 1) == me * rows + iota((128 * rows, length), 0) // 128)
-        mask_all = (dot_nt(mk, picks.astype(F32).astype(BF16)) - 1.0) * (MASK_SCALE * LOG2E)
+        mask_all = (dot_nt(mk, mine) - 1.0) * (MASK_SCALE * LOG2E)
         for i in range(rows):
-            mc_s[i] = mask_all[:, seg(i, 128)]
+            mc_s[i] = jnp.broadcast_to(mask_all[:, i:i + 1], (n_seq, 128))
         tokens = 4 * n_seq
 
         def doubled(y):
@@ -341,7 +338,7 @@
         @pl.when(c == 1)
         def _():
             gather_relay(g_c, 2, 0, near)
-            send_back(0, near + far[:2])
+            send_back(0, middle_hops)
 
         def middle(q):
             zeros = jnp.zeros((64, 128), BF16)
@@ -366,7 +363,7 @@
             update = dot_tn(oc_s[q], w_co[:])
             x = y1[pl.ds(4 * q, 4)].reshape(tokens, width).astype(F32)
             y1[pl.ds(4 * q, 4)] = (x + update).astype(BF16).reshape(4, n_seq, width)
-        loop(quads, after, U_CA)
+        loop(quads, after, U_CF)
 
         @pl.when(c == 1)
         def _():
@@ -392,6 +389,14 @@
             part = y1[:, seg(db, 16), :].reshape(16 * rows, width)
             s2[c, seg(db, sup), :] = dot(p3t[:], part).astype(BF16)
         exchange_own(s2, r2, lambda d: (c, rows_of(d)))
+
+        @pl.when(c == 0)
+        def _():
+            send_back(0, near)
+
+        @pl.when(c == 1)
+        def _():
+            send_back(0, last_hops)
     loop(crops, columns)
 
     def bias_row(i, y, w_b):
@@ -425,7 +430,7 @@
 
         @pl.when(c == 1)
         def _():
-            send_back(1, near + far[:2])
+            send_back(1, last_hops)
 
         def one(i):
             update = dot(w_fet[:], u_s[i])
@@ -435,6 +440,7 @@
         @pl.when(c == 0)
         def _():
             gather_relay(g_c, 2, 1, near)
+            send_back(1, near)
 
         def norm(i):
             y = layer_norm(z1[c, i])
@@ -447,7 +453,10 @@
             start_project(0)
             relay_forward(g_c, 2, 1)
         bias_send(g_t1, 3, c, steps)
-        send_back(c, far[2:] + (0,))
+
+        @pl.when(c == 0)
+        def _():
+            send_back(1, middle_hops)
 
         @pl.when(c == 1)
         def _():

time: 158 us -> 148 us (0.937)
  Pallas kernels: 153 us -> 144 us
    pallas_call x1, Pallas kernels: 153 us -> 144 us  [local_block(): pl.pallas_call(functools.partial(block_kernel, n), out_shape=(jax.ShapeDt...]
where the time goes in v5:
time: 148 us; the launch traced here: 147 us
  Pallas kernels  144 us (97%)
  local copies, waits for them, and re-layouts  3.18 us (2%)
    pallas_call x1, Pallas kernels, local_block(): pl.pallas_call(functools.partial(block_kernel, n), out_shape=(jax.ShapeDt...  144 us
    unnamed x4, local copies, waits for them, and re-layouts  3.18 us

profile of v5, /device:TPU:21, one launch (start us, length us, event | category | flops | bytes accessed | tf_op | source)
XLA Modules:
  0.0 147.3 jit_solution(16305682225618441996)
XLA Ops:
  0.6 143.5 %evoformer_block.1 = (bf16[2,4,192,256]{3,2,1,0:T(8,128)(2,1)}, bf16[2,12,192,128]{3,2,1,0:T(8,128)(2,1)}) custom-call(bf16[2,4,192,256]{3,2,1,0:T(8,128)(2,1)} %x_ref.1, bf16[2,12,192,128]{3,2,1,0:T(8,128)(2,1)} %z_ref.1, s32[2,64,192]{2,1,0:T(8,128)} %mm_ref.1, s32[2,192]{1,0:T(2,128)} %rm_ref.1, bf16[8,128]{1,0:T(8,128)(2,1)} %bitcast.33, ...), custom_call_target="tpu_custom_call" | custom-call | tf_op jit(solution)/shard_map/evoformer_block/pallas_call | solution.py:641
  144.2 0.0 copy-start
  144.2 2.2 %copy.36 = bf16[2,4,192,256]{3,2,1,0:T(8,128)(2,1)} copy(bf16[2,4,192,256]{3,2,1,0:T(8,128)(2,1)} %get-tuple-element.4) | data formatting | bytes 1572864
  146.3 0.0 copy-done
  146.3 1.0 copy.37
Async XLA Ops:
  144.2 2.2 %copy-start = (bf16[2,12,192,128]{3,2,1,0:T(8,128)(2,1)S(1)}, bf16[2,12,192,128]{3,2,1,0:T(8,128)(2,1)}, u32[]{:S(2)}) copy-start(bf16[2,12,192,128]{3,2,1,0:T(8,128)(2,1)} %get-tuple-element.5) | copy-start | bytes 3538948

commit v6 on v5

--- a/solution.py
+++ b/solution.py
@@ -26,7 +26,7 @@
 
 
 def dot(a, b):
-    return lax.dot_general(a, b, (((1,), (0,)), ((), ())), preferred_element_type=F32)
+    return lax.dot(a, b, preferred_element_type=F32)
 
 
 def dot_nt(a, b):
@@ -73,7 +73,23 @@
     return (iota((width, lanes), 0) // HD) % 2 == (iota((width, lanes), 1) // half) % 2
 
 
-def block_kernel(n, x_ref, z_ref, mm_ref, rm_ref,
+def staged_kernel(n, early, n_in, *refs):
+    operands, rest = list(refs[:n_in]), refs[n_in:]
+    late = [i for i in range(n_in) if i not in early]
+    landing, sems = rest[-len(late) - 1:-1], rest[-1]
+    copies = [pltpu.make_async_copy(operands[i], landing[k], sems.at[k]) for k, i in enumerate(late)]
+    for copy in copies:
+        copy.start()
+    for k, i in enumerate(late):
+        operands[i] = landing[k]
+
+    def arrive():
+        for copy in copies:
+            copy.wait()
+    block_kernel(n, arrive, *operands, *rest[:-len(late) - 1])
+
+
+def block_kernel(n, arrive, x_ref, z_ref, mm_ref, rm_ref,
                  w_rb, w_r, w_ro, w_c, w_co, w_ac, w_oo, w_tsb, w_ts, w_tso, w_teb, w_te, w_teo,
                  p2, p2t, p3, p3t, p4, p4b, p4e, p4eb, p5, p6, p64, eye, tok, tok_l, tok_r,
                  out_m, out_z,
@@ -94,8 +110,8 @@
     blk = 4 * rows
     sup = 4 * blk
     steps = []
-    for k in range(chips // 2, 0, -1):
-        steps += [k] if chips - k == k else [chips - k, k]
+    for k in reversed(range(chips // 2)):
+        steps += sorted({k + 1, chips - k - 1}, reverse=True)
     near = (2, chips - 2, 1, chips - 1)
     far = tuple(k for k in steps if k not in near)
     middle_hops, last_hops = far[1:], far[:1] + (0,)
@@ -205,6 +221,7 @@
             buf[c, me] = pack_bias(t[seg(g, blk), :])
     loop(crops, row_bias)
     pl.semaphore_wait(barrier, n - 1)
+    arrive()
 
     def row_bias_send(c):
         for g, buf in enumerate(g_row):
@@ -364,10 +381,6 @@
             x = y1[pl.ds(4 * q, 4)].reshape(tokens, width).astype(F32)
             y1[pl.ds(4 * q, 4)] = (x + update).astype(BF16).reshape(4, n_seq, width)
         loop(quads, after, U_CF)
-
-        @pl.when(c == 1)
-        def _():
-            relay_forward(g_c, 2, 0)
 
         def factors(q):
             y = layer_norm(y1[pl.ds(4 * q, 4)].reshape(tokens, width))
@@ -410,6 +423,9 @@
         loop(rows, lambda i: project(yn[c, i], w_ts, i), U_TP)
 
     def outer(c):
+        @pl.when(c == 0)
+        def _():
+            relay_forward(g_c, 2, 0)
         gather_wait(g_c, 2, c)
 
         def unpack(q):
@@ -462,6 +478,9 @@
         def _():
             gather_forward(g_t1, 3, 0, steps)
     loop(crops, outer)
+
+    def relay_bias_at(turn, q, c):
+        pl.when(turn & (q == 0))(lambda: gather_relay(g_t2, 4, c, near))
 
     def triangle(c, w_out, done):
         def quad(q):
@@ -493,10 +512,11 @@
 
             @pl.when(q == quads - 1)
             def _():
-                bias_send(g_t2, 4, c, steps)
+                bias_send(g_t2, 4, c, near)
             for b in range(blocks):
                 part = x3[pl.ds(4 * q, 4), seg(b, 64), :].reshape(256, 128)
                 s3[c, q, seg(b, 256), :] = dot(p2[:], part).astype(BF16)
+            relay_bias_at(c == 1, q, 0)
             exchange_start(s3, r3, 2, c, lambda d: (c, q, rows_of(d)))
         triangle(c, w_tso, done)
     loop(crops, start_node)
@@ -510,7 +530,7 @@
                     at = 64 * q + 16 * sb
                     z1[c, i, at:at + 16, :] = moved[seg(i, 16), :]
         loop(rows, lambda i: project(layer_norm(z1[c, i]), w_te, i), U_TP)
-        gather_forward(g_t2, 4, c, steps)
+        relay_forward(g_t2, 4, c)
         gather_wait(g_t2, 4, c)
         unpack_bias(g_t2, c, p4e, p4eb, 4 * quads, 16)
         col = mask_columns(rm_ref[pl.ds(c, 1), :], tok)
@@ -527,6 +547,7 @@
                     moved = dot(p64[:], part).astype(BF16)
                     for i in range(4):
                         s4[c, p, rows_of(4 * db + i, 16 * q, 16), :] = moved[seg(i, 16), :]
+            relay_bias_at(c == 0, q, 1)
             exchange_start(s4, r4, 3, c, lambda d: (c, slice(None), rows_of(d, 16 * q, 16)))
         triangle(c, w_teo, done)
     loop(crops, end_node)
@@ -549,7 +570,7 @@
     loop(crops, finish_pair)
 
     def drain(c):
-        for e, (buf, hops) in enumerate([(b, steps) for b in g_row] + [(g_c, near), (g_t1, steps), (g_t2, steps)]):
+        for e, (buf, hops) in enumerate([(b, steps) for b in g_row] + [(g_c, near), (g_t1, steps), (g_t2, near)]):
             gather_end(buf, e, c, hops)
         for e, (buf, planes) in enumerate(((s1, False), (s2, False), (s3, True), (s4, True))):
             exchange_end(buf, e, c, planes)
@@ -558,8 +579,8 @@
 
 def solution(mesh):
     n = mesh.shape[GROUP_AXIS]
-    rows_spec = P(PART_AXIS, GROUP_AXIS, None, None)
-    in_specs = (rows_spec, rows_spec, P(PART_AXIS, None, None), P(PART_AXIS, None)) + (P(),) * N_WEIGHTS
+    rows_spec = P(PART_AXIS, GROUP_AXIS)
+    in_specs = (rows_spec, rows_spec, P(PART_AXIS), P(PART_AXIS)) + (P(),) * N_WEIGHTS
 
     def local_block(msa, pair, msa_mask, res_mask, *weights):
         (w_rb, w_r, w_ro, w_c, w_co, w_ac, w_oo, w_tsb, w_ts, w_tso, w_teb, w_te, w_teo) = weights
@@ -572,9 +593,10 @@
         def flat_t(w):
             return jnp.transpose(w, (1, 2, 3, 0)).reshape(-1, w.shape[0])
 
+        bias_t = w_rb.T
         operands = [
             msa, pair, msa_mask, res_mask,
-            w_rb.T, flat_t(w_r), w_ro.reshape(width, width), flat_t(w_c), w_co.reshape(width, width),
+            bias_t, flat_t(w_r), w_ro.reshape(width, width), flat_t(w_c), w_co.reshape(width, width),
             jnp.transpose(w_ac, (1, 2, 0)).reshape(-1, width), w_oo.reshape(-1, pair_width),
             w_tsb.T, flat_t(w_ts), w_tso.reshape(pair_width, pair_width),
             w_teb.T, flat_t(w_te), w_teo.reshape(pair_width, pair_width),
@@ -586,16 +608,20 @@
 
         def last(p):
             half = p[:len(p) // 2].reshape(-1, 4, 4 * rows)[:, :, :2 * rows]
-            return np.pad(half, ((0, 0), (0, 0), (0, 32 - 2 * rows))).reshape(len(p) // 2, -1)
+            blank = np.zeros(half.shape[:2] + (32 - 2 * rows,))
+            return np.concatenate([half, blank], axis=2).reshape(len(half), -1)
         p5 = permutation((rows, HD // 2), (1, 0))
         p6 = permutation((rows, heads), (1, 0))
         p64 = permutation((4, 4, 4), (1, 0, 2))
         tok = permutation((n, quads, 4), (1, 0, 2))
         consts = [p2, p2.T, p3, p3.T, p4, last(p4), p4e, last(p4e), p5, p6, p64, np.eye(length), tok,
                   np.concatenate([tok, 0 * tok]), np.concatenate([0 * tok, tok])]
+        first_const, names = len(operands), [a is p6 for a in consts]
         operands += [jnp.asarray(a, BF16) for a in consts]
 
         vmem = pl.BlockSpec(memory_space=pltpu.VMEM)
+        anywhere = pl.BlockSpec(memory_space=pl.ANY)
+        early = tuple(i for i, a in enumerate(operands) if a is pair or a is bias_t or (i >= first_const and names[i - first_const]))
         total = n * 4 * rows
         bias = pltpu.VMEM((crops, n, 4 * rows + 32, 128), BF16)
         scratch = [
@@ -638,10 +664,12 @@
             pltpu.VMEM((rows, n_seq, 128), F32),
         ]
         scratch += [pltpu.SemaphoreType.DMA((5, crops))] * 8
+        late = [a for i, a in enumerate(operands) if i not in early]
+        scratch += [pltpu.VMEM(a.shape, a.dtype) for a in late] + [pltpu.SemaphoreType.DMA((len(late),))]
         return pl.pallas_call(
-            functools.partial(block_kernel, n),
+            functools.partial(staged_kernel, n, early, len(operands)),
             out_shape=(jax.ShapeDtypeStruct(msa.shape, BF16), jax.ShapeDtypeStruct(pair.shape, BF16)),
-            in_specs=[vmem] * len(operands),
+            in_specs=[vmem if i in early else anywhere for i in range(len(operands))],
             out_specs=(vmem, vmem),
             scratch_shapes=scratch,
             compiler_params=pltpu.CompilerParams(collective_id=0, has_side_effects=True, vmem_limit_bytes=VMEM_BYTES),

time: 148 us -> 145 us (0.980)
  Pallas kernels: 144 us -> 141 us
    pallas_call x1, Pallas kernels: 144 us -> 141 us  [local_block(): pl.pallas_call(functools.partial(staged_kernel, n, early, len(operands)),...]
where the time goes in v6:
time: 145 us
  Pallas kernels  141 us (97%)
  local copies, waits for them, and re-layouts  3.18 us (2%)
    pallas_call x1, Pallas kernels, local_block(): pl.pallas_call(functools.partial(staged_kernel, n, early, len(operands)),...  141 us
    unnamed x4, local copies, waits for them, and re-layouts  3.18 us

profile of v6, /device:TPU:21, one launch (start us, length us, event | category | flops | bytes accessed | tf_op | source)
XLA Modules:
  0.0 145.3 jit_solution(9658017947818899744)
XLA Ops:
  0.6 141.4 %evoformer_block.1 = (bf16[2,4,192,256]{3,2,1,0:T(8,128)(2,1)}, bf16[2,12,192,128]{3,2,1,0:T(8,128)(2,1)}) custom-call(bf16[2,4,192,256]{3,2,1,0:T(8,128)(2,1)} %refs_0_.1, bf16[2,12,192,128]{3,2,1,0:T(8,128)(2,1)} %refs_1_.1, s32[2,64,192]{2,1,0:T(8,128)} %refs_2_.1, s32[2,192]{1,0:T(2,128)} %refs_3_.1, bf16[8,128]{1,0:T(8,128)(2,1)} %bitcast.33, ...), custom_call_target="tpu_custom_call" | custom-call | tf_op jit(solution)/shard_map/evoformer_block/pallas_call | solution.py:669
  142.1 0.0 copy-start
  142.1 2.2 %copy.36 = bf16[2,4,192,256]{3,2,1,0:T(8,128)(2,1)} copy(bf16[2,4,192,256]{3,2,1,0:T(8,128)(2,1)} %get-tuple-element.4) | data formatting | bytes 1572864
  144.2 0.0 copy-done
  144.2 1.0 copy.37
Async XLA Ops:
  142.1 2.2 %copy-start = (bf16[2,12,192,128]{3,2,1,0:T(8,128)(2,1)S(1)}, bf16[2,12,192,128]{3,2,1,0:T(8,128)(2,1)}, u32[]{:S(2)}) copy-start(bf16[2,12,192,128]{3,2,1,0:T(8,128)(2,1)} %get-tuple-element.5) | copy-start | bytes 3538948

commit v7 on v6

--- a/solution.py
+++ b/solution.py
@@ -226,7 +226,7 @@
     def row_bias_send(c):
         for g, buf in enumerate(g_row):
             gather_start(buf, g, c, steps)
-    loop(crops, row_bias_send)
+    row_bias_send(0)
 
     w_f32[:] = w_oo[:].astype(F32)
     for fp in range(HD // 2):
@@ -299,6 +299,7 @@
             m_s[s] = mask_columns(mm_ref[c, pl.ds(me * seqs + s, 1), :], eye)
             project(layer_norm(x_ref[c, s]), w_r, s, seqs)
         loop(seqs, before, U_PR)
+        pl.when(c == 0)(lambda: row_bias_send(1))
         for g, buf in enumerate(g_row):
             gather_forward(buf, g, c, steps)
             gather_wait(buf, g, c)
@@ -516,8 +517,8 @@
             for b in range(blocks):
                 part = x3[pl.ds(4 * q, 4), seg(b, 64), :].reshape(256, 128)
                 s3[c, q, seg(b, 256), :] = dot(p2[:], part).astype(BF16)
+            exchange_start(s3, r3, 2, c, lambda d: (c, q, rows_of(d)))
             relay_bias_at(c == 1, q, 0)
-            exchange_start(s3, r3, 2, c, lambda d: (c, q, rows_of(d)))
         triangle(c, w_tso, done)
     loop(crops, start_node)
 

time: 145 us -> 145 us (level)
  no operation moved by 1% of the time
where the time goes in v7:
time: 145 us
  Pallas kernels  141 us (97%)
  local copies, waits for them, and re-layouts  3.18 us (2%)
    pallas_call x1, Pallas kernels, local_block(): pl.pallas_call(functools.partial(staged_kernel, n, early, len(operands)),...  141 us
    unnamed x4, local copies, waits for them, and re-layouts  3.18 us

profile of v7, /device:TPU:21, one launch (start us, length us, event | category | flops | bytes accessed | tf_op | source)
XLA Modules:
  0.0 144.8 jit_solution(13265954082633685160)
XLA Ops:
  0.6 140.9 %evoformer_block.1 = (bf16[2,4,192,256]{3,2,1,0:T(8,128)(2,1)}, bf16[2,12,192,128]{3,2,1,0:T(8,128)(2,1)}) custom-call(bf16[2,4,192,256]{3,2,1,0:T(8,128)(2,1)} %refs_0_.1, bf16[2,12,192,128]{3,2,1,0:T(8,128)(2,1)} %refs_1_.1, s32[2,64,192]{2,1,0:T(8,128)} %refs_2_.1, s32[2,192]{1,0:T(2,128)} %refs_3_.1, bf16[8,128]{1,0:T(8,128)(2,1)} %bitcast.33, ...), custom_call_target="tpu_custom_call" | custom-call | tf_op jit(solution)/shard_map/evoformer_block/pallas_call | solution.py:670
  141.6 0.0 copy-start
  141.6 2.2 %copy.36 = bf16[2,4,192,256]{3,2,1,0:T(8,128)(2,1)} copy(bf16[2,4,192,256]{3,2,1,0:T(8,128)(2,1)} %get-tuple-element.4) | data formatting | bytes 1572864
  143.8 0.0 copy-done
  143.8 1.0 copy.37
Async XLA Ops:
  141.6 2.2 %copy-start = (bf16[2,12,192,128]{3,2,1,0:T(8,128)(2,1)S(1)}, bf16[2,12,192,128]{3,2,1,0:T(8,128)(2,1)}, u32[]{:S(2)}) copy-start(bf16[2,12,192,128]{3,2,1,0:T(8,128)(2,1)} %get-tuple-element.5) | copy-start | bytes 3538948
